TPU v7x, 8 devices: a whole 2x2x1 slice. The times are simulated.
8 devices in a mesh: dp: 1 (over z), x: 2 (over y), y: 4 (over x, core).
Axes of the slice: x: 2, y: 2, z: 1, core: 2. Of those that a mesh axis runs over, the one named last changes fastest.
Arguments:
- hidden: bfloat16 [1024, 2048], P('dp', 'x')
- w_qkv: bfloat16 [2048, 6144], P('x', 'y')
- b_qkv: bfloat16 [6144], P('y')
- w_out: bfloat16 [2048, 2048], P('y', 'x')
- b_out: bfloat16 [2048], P('x')
- attn_gain: bfloat16 [2048], P('x')
- attn_shift: bfloat16 [2048], P('x')
- w_up: bfloat16 [2048, 2, 8192], P('x', None, 'y')
- b_up: bfloat16 [2, 8192], P(None, 'y')
- w_down: bfloat16 [8192, 2048], P('y', 'x')
- b_down: bfloat16 [2048], P('x')
- mlp_gain: bfloat16 [2048], P('x')
- mlp_shift: bfloat16 [2048], P('x')
- k_cache: bfloat16 [1024, 64, 32, 64], P('dp', None, 'y')
- v_cache: bfloat16 [1024, 64, 32, 64], P('dp', None, 'y')
- positions: int32 [1024], P('dp')
- lengths: int32 [1024], P('dp')
Outputs:
- output 1: bfloat16 [1024, 2048], P('dp', 'x')
- output 2: bfloat16 [1024, 64, 32, 64], P('dp', None, 'y')
- output 3: bfloat16 [1024, 64, 32, 64], P('dp', None, 'y')
All inputs are finite; a program needn't handle non-finite values.
Results may differ from a plain program's by a relative error of at most 0.02.
Values are sent between devices in bfloat16 or wider.
A program may use at most 1.25 GiB of HBM per device.

v0:
```python
import math
import jax
import jax.numpy as jnp
from jax import lax
from jax.sharding import PartitionSpec as P

DEEP_ALPHA = math.sqrt(140.0)
LN_EPS = 1e-5
ROPE_BASE = 10000.0


def apply_rotary(head_vec, positions):
    head_dim = head_vec.shape[-1]
    half_dim = head_dim // 2
    inv_freq = ROPE_BASE ** (-2.0 * jnp.arange(half_dim, dtype=jnp.float32) / head_dim)
    angles = positions.astype(jnp.float32)[:, None] * inv_freq[None, :]
    cos_table = jnp.cos(angles)[:, None, :]
    sin_table = jnp.sin(angles)[:, None, :]
    vec_wide = head_vec.astype(jnp.float32)
    lower_half = vec_wide[..., :half_dim]
    upper_half = vec_wide[..., half_dim:]
    return jnp.concatenate([lower_half * cos_table - upper_half * sin_table, upper_half * cos_table + lower_half * sin_table], axis=-1).astype(jnp.bfloat16)


def write_slot(cache, new_rows, lengths):
    slot_hit = jnp.arange(cache.shape[1])[None, :, None, None] == lengths[:, None, None, None]
    return jnp.where(slot_hit, new_rows[:, None], cache)


def attend(query_rot, k_full, v_full, lengths):
    head_dim = query_rot.shape[-1]
    scores = jnp.einsum('bhd,bshd->bhs', query_rot, k_full, preferred_element_type=jnp.float32) * (head_dim ** -0.5)
    slot_ok = jnp.arange(k_full.shape[1])[None, None, :] <= lengths[:, None, None]
    scores = jnp.where(slot_ok, scores, -1e30)
    attn_probs = jax.nn.softmax(scores, axis=-1).astype(jnp.bfloat16)
    attn_mixed = jnp.einsum('bhs,bshd->bhd', attn_probs, v_full, preferred_element_type=jnp.float32)
    return attn_mixed.astype(jnp.bfloat16).reshape(query_rot.shape[0], -1)


def sharded_norm(h_val, gain, shift, width_all):
    moments = jnp.stack([jnp.sum(h_val, axis=1), jnp.sum(h_val * h_val, axis=1)], axis=1)
    moments = lax.psum(moments, 'x')
    mean_row = moments[:, 0:1] / width_all
    var_row = moments[:, 1:2] / width_all - mean_row * mean_row
    scaled = (h_val - mean_row) * lax.rsqrt(var_row + LN_EPS)
    return (scaled * gain.astype(jnp.float32) + shift.astype(jnp.float32)).astype(jnp.bfloat16)


def solution(mesh):
    x_size = mesh.shape['x']
    cache_spec = P('dp', None, 'y', None)
    width_spec = P('x')
    in_specs = (P('dp', 'x'), P('x', 'y'), P('y'), P('y', 'x'), width_spec, width_spec, width_spec, P('x', None, 'y'), P(None, 'y'), P('y', 'x'), width_spec, width_spec, width_spec, cache_spec, cache_spec, P('dp'), P('dp'))
    out_specs = (P('dp', 'x'), cache_spec, cache_spec)

    def local_step(hidden, w_qkv, b_qkv, w_out, b_out, attn_gain, attn_shift, w_up, b_up, w_down, b_down, mlp_gain, mlp_shift, k_cache, v_cache, positions, lengths):
        row_count, width_local = hidden.shape
        width_all = width_local * x_size
        local_heads, head_dim = k_cache.shape[2], k_cache.shape[3]
        qkv_part = jnp.dot(hidden, w_qkv, preferred_element_type=jnp.float32).astype(jnp.bfloat16)
        qkv_sum = lax.psum(qkv_part, 'x')
        qkv_vals = (qkv_sum.astype(jnp.float32) + b_qkv.astype(jnp.float32)).astype(jnp.bfloat16)
        qkv_vals = qkv_vals.reshape(row_count, local_heads, 3, head_dim)
        query_rot = apply_rotary(qkv_vals[:, :, 0], positions)
        k_full = write_slot(k_cache, apply_rotary(qkv_vals[:, :, 1], positions), lengths)
        v_full = write_slot(v_cache, qkv_vals[:, :, 2], lengths)
        attn_out = attend(query_rot, k_full, v_full, lengths)
        proj_part = jnp.dot(attn_out, w_out, preferred_element_type=jnp.float32).astype(jnp.bfloat16)
        proj_sum = lax.psum(proj_part, 'y')
        h_attn = DEEP_ALPHA * hidden.astype(jnp.float32) + proj_sum.astype(jnp.float32) + b_out.astype(jnp.float32)
        normed = sharded_norm(h_attn, attn_gain, attn_shift, width_all)
        up_part = jnp.einsum('bd,dtf->btf', normed, w_up, preferred_element_type=jnp.float32).astype(jnp.bfloat16)
        up_sum = lax.psum(up_part, 'x').astype(jnp.float32) + b_up.astype(jnp.float32)
        gated_act = (jax.nn.gelu(up_sum[:, 0], approximate=True) * up_sum[:, 1]).astype(jnp.bfloat16)
        down_part = jnp.dot(gated_act, w_down, preferred_element_type=jnp.float32).astype(jnp.bfloat16)
        down_sum = lax.psum(down_part, 'y')
        h_mlp = DEEP_ALPHA * normed.astype(jnp.float32) + down_sum.astype(jnp.float32) + b_down.astype(jnp.float32)
        result = sharded_norm(h_mlp, mlp_gain, mlp_shift, width_all)
        return result, k_full, v_full

    return jax.shard_map(local_step, mesh=mesh, in_specs=in_specs, out_specs=out_specs, check_vma=False)
```

profile of v0, /device:TPU:0, one launch (start us, length us, event | category | flops | bytes accessed | tf_op | source)
XLA Modules:
  0.0 586.6 jit_solution(7037630409111464539)
XLA Ops:
  7.2 0.0 copy-start
  7.2 0.0 copy-start.6
  7.2 0.0 copy-start.8
  7.2 0.0 copy-start.7
  7.2 0.0 all-reduce.5.cloned.1.call-start
  7.3 1.8 copy-done
  9.1 6.3 %convolution_convert_fusion = bf16[1024,1536]{1,0:T(8,128)(2,1)} fusion(bf16[1024,1024]{1,0:T(8,128)(2,1)} %param.17, bf16[1024,1536]{1,0:T(8,128)(2,1)S(1)} %copy-done), kind=kOutput, calls=%fused_computation.30 | convolution fusion | flops 3222798336 | bytes 8388608 | tf_op jit(solution)/shard_map/dot_general | solution.py:60
  15.4 0.0 all-reduce.5.cloned.1.call-update
  15.4 0.0 all-reduce.7.cloned.1.call-start
  15.5 0.0 copy-done.6
  15.5 0.0 copy-done.8
  15.5 0.0 copy-done.7
  15.6 0.1 iota_compare_fusion.1
  15.6 0.5 multiply_cosine_fusion
  16.2 82.2 %all-reduce.5.cloned.1.call-done = bf16[1024,1536]{1,0:T(8,128)(2,1)} async-done(((bf16[1024,1536]{1,0:T(8,128)(2,1)}), bf16[1024,1536]{1,0:T(8,128)(2,1)}) %all-reduce.5.cloned.1.call-update) | async-done | bytes 3145744 | tf_op jit(solution)/shard_map/psum | solution.py:61
  98.4 2.5 add_convert_fusion
  100.8 2.9 copy.29
  103.7 3.4 slice_bitcast_fusion.2
  107.1 0.6 subtract_convert_fusion
  107.7 0.3 maximum_convert_fusion
  108.1 58.9 %multiply_reduce_fusion.1 = (f32[1024,8,64]{0,1,2:T(8,128)}, bf16[1024,64,8,64]{0,3,2,1:T(8,128)(2,1)}) fusion(f32[1024,8,64]{0,2,1:T(8,128)S(1)} %get-tuple-element.28, bf16[1024,64,8,64]{0,3,2,1:T(8,128)(2,1)} %param.30, bf16[1024,8,64]{0,2,1:T(8,128)(2,1)S(1)} %get-tuple-element.29, pred[1024,64]{0,1:T(8,128)(4,1)S(1)} %get-tuple-element.27), kind=kLoop, calls=%fused_computation.3 | loop fusion | flops 133693440 | bytes 139526144
  166.9 4.9 fusion.27
  171.9 0.0 copy-start.4
  171.9 2.9 copy.47
  174.8 0.0 copy-done.4
  174.8 46.5 %multiply_reduce_fusion = (bf16[1024,8,64]{0,2,1:T(8,128)(2,1)}, bf16[1024,64,8,64]{0,3,2,1:T(8,128)(2,1)}) fusion(f32[1024,8,64]{0,1,2:T(8,128)S(1)} %copy.47, bf16[1024,64,8,64]{0,3,2,1:T(8,128)(2,1)} %param.31, bf16[1024,8,64]{0,2,1:T(8,128)(2,1)S(1)} %copy-done.4, pred[1024,64]{0,1:T(8,128)(4,1)S(1)} %get-tuple-element.27), kind=kLoop, calls=%fused_computation.2 | loop fusion | flops 133693440 | bytes 138477568 | tf_op jit(solution)/shard_map/bhs,bshd->bhd/dot_general | solution.py:36
  221.3 0.0 copy-start.9
  221.3 0.0 copy-start.10
  221.3 0.0 copy-start.11
  221.3 0.0 copy-start.3
  221.3 4.3 convolution_convert_fusion.1
  225.6 0.0 all-reduce.7.cloned.1.call-update
  225.6 0.0 all-reduce.9.cloned.1.call-start
  225.7 0.0 copy-done.9
  225.7 0.0 copy-done.10
  225.7 0.0 copy-done.11
  225.7 45.7 %all-reduce.7.cloned.1.call-done = bf16[1024,1024]{1,0:T(8,128)(2,1)} async-done(((bf16[1024,1024]{1,0:T(8,128)(2,1)}), bf16[1024,1024]{1,0:T(8,128)(2,1)}) %all-reduce.7.cloned.1.call-update) | async-done | bytes 2097168 | tf_op jit(solution)/shard_map/psum | solution.py:69
  271.4 0.0 copy-done.3
  271.4 2.8 fusion.18
  274.2 5.0 psum.44
  279.2 3.0 add_convert_fusion.2
  282.3 0.0 copy-start.2
  282.3 23.7 %fusion.13 = bf16[1024,2,2048]{2,0,1:T(8,128)(2,1)} fusion(bf16[1024,2,2048]{2,1,0:T(2,128)(2,1)} %param.24, bf16[1024,1024]{1,0:T(8,128)(2,1)S(1)} %add_convert_fusion.2), kind=kOutput, calls=%fused_computation.22 | convolution fusion | flops 8594128896 | bytes 18874368 | tf_op jit(solution)/shard_map/bd,dtf->btf/dot_general | solution.py:72
  305.9 0.0 copy-done.2
  305.9 0.0 copy-start.5
  306.0 0.0 all-reduce.9.cloned.1.call-update
  306.0 0.0 all-reduce.11.cloned.1.call-start
  306.0 0.6 copy-done.5
  306.7 191.8 %all-reduce.9.cloned.1.call-done = bf16[1024,2,2048]{2,0,1:T(8,128)(2,1)} async-done(((bf16[1024,2,2048]{2,0,1:T(8,128)(2,1)}), bf16[1024,2,2048]{2,0,1:T(8,128)(2,1)}) %all-reduce.9.cloned.1.call-update) | async-done | bytes 8388624 | tf_op jit(solution)/shard_map/psum | solution.py:73
  498.4 11.5 %convert_add_fusion = f32[1024,2,2048]{2,0,1:T(8,128)} fusion(bf16[1024,2,2048]{2,0,1:T(8,128)(2,1)} %all-reduce.9.cloned.1.call-done, f32[2,2048]{1,0:T(2,128)S(1)} %convert_element_type.115), kind=kLoop, calls=%fused_computation.6 | loop fusion | flops 8388608 | bytes 25182208 | tf_op jit(solution)/shard_map/add | solution.py:73
  509.9 0.0 copy-start.12
  509.9 0.0 copy-start.13
  509.9 0.0 copy-start.14
  509.9 11.3 %fusion.22 = bf16[1024,1024]{1,0:T(8,128)(2,1)} fusion(bf16[2048,1024]{1,0:T(8,128)(2,1)} %param.26, f32[1024,2,2048]{2,0,1:T(8,128)} %convert_add_fusion), kind=kOutput, calls=%fused_computation.39 | convolution fusion | flops 4316987392 | bytes 23068672 | tf_op jit(solution)/shard_map/dot_general | solution.py:75
  521.2 0.0 all-reduce.11.cloned.1.call-update
  521.2 0.0 copy-done.12
  521.3 0.0 copy-done.13
  521.3 0.0 copy-done.14
  521.3 46.1 %all-reduce.11.cloned.1.call-done = bf16[1024,1024]{1,0:T(8,128)(2,1)} async-done(((bf16[1024,1024]{1,0:T(8,128)(2,1)}), bf16[1024,1024]{1,0:T(8,128)(2,1)}) %all-reduce.11.cloned.1.call-update) | async-done | bytes 2097168 | tf_op jit(solution)/shard_map/psum | solution.py:76
  567.4 0.0 copy-start.1
  567.4 3.6 fusion.19
  571.0 5.0 psum.47
  576.0 4.0 add_convert_fusion.1
  580.0 0.0 copy-done.1
  (14 shorter events, 0.1 us)
Async XLA Ops:
  7.2 1.9 copy-start
  7.2 8.3 %copy-start.6 = (bf16[1536]{0:T(1024)(128)(2,1)S(1)}, bf16[1536]{0:T(1024)(128)(2,1)}, u32[]{:S(2)}) copy-start(bf16[1536]{0:T(1024)(128)(2,1)} %param.19) | copy-start | bytes 9220
  7.2 8.3 %copy-start.8 = (s32[1024]{0:T(1024)S(1)}, s32[1024]{0:T(1024)}, u32[]{:S(2)}) copy-start(s32[1024]{0:T(1024)} %param.32) | copy-start | bytes 12292
  7.2 8.3 %copy-start.7 = (s32[1024]{0:T(1024)S(1)}, s32[1024]{0:T(1024)}, u32[]{:S(2)}) copy-start(s32[1024]{0:T(1024)} %param.33) | copy-start | bytes 12292
  7.2 91.2 %all-reduce.5.cloned.1.call-start = ((), (), s32[]{:S(2)}) async-start(), calls=%async_computation | async-start | bytes 6291456 | tf_op jit(solution)/shard_map/psum | solution.py:61
  15.4 256.0 %all-reduce.7.cloned.1.call-start = ((), (), s32[]{:S(2)}) async-start(), calls=%async_computation.1 | async-start | bytes 4194304 | tf_op jit(solution)/shard_map/psum | solution.py:69
  171.9 2.9 copy-start.4
  221.3 4.4 copy-start.9
  221.3 4.4 copy-start.10
  221.3 4.4 copy-start.11
  221.3 50.1 %copy-start.3 = (bf16[1024,1024]{1,0:T(8,128)(2,1)S(1)}, bf16[1024,1024]{1,0:T(8,128)(2,1)}, u32[]{:S(2)}) copy-start(bf16[1024,1024]{1,0:T(8,128)(2,1)} %param.17) | copy-start | bytes 6291460
  225.6 272.8 %all-reduce.9.cloned.1.call-start = ((), (), s32[]{:S(2)}) async-start(), calls=%async_computation.2 | async-start | bytes 16777216 | tf_op jit(solution)/shard_map/psum | solution.py:73
  282.3 23.7 %copy-start.2 = (bf16[1024,1024]{1,0:T(8,128)(2,1)}, bf16[1024,1024]{1,0:T(8,128)(2,1)S(1)}, u32[]{:S(2)}) copy-start(bf16[1024,1024]{1,0:T(8,128)(2,1)S(1)} %add_convert_fusion.2) | copy-start | bytes 6291460
  305.9 0.7 copy-start.5
  306.0 261.4 %all-reduce.11.cloned.1.call-start = ((), (), s32[]{:S(2)}) async-start(), calls=%async_computation.3 | async-start | bytes 4194304 | tf_op jit(solution)/shard_map/psum | solution.py:76
  509.9 11.3 %copy-start.12 = (bf16[1024]{0:T(1024)(128)(2,1)S(1)}, bf16[1024]{0:T(1024)(128)(2,1)}, u32[]{:S(2)}) copy-start(bf16[1024]{0:T(1024)(128)(2,1)} %param.27) | copy-start | bytes 6148
  509.9 11.3 %copy-start.13 = (bf16[1024]{0:T(1024)(128)(2,1)S(1)}, bf16[1024]{0:T(1024)(128)(2,1)}, u32[]{:S(2)}) copy-start(bf16[1024]{0:T(1024)(128)(2,1)} %param.28) | copy-start | bytes 6148
  509.9 11.3 %copy-start.14 = (bf16[1024]{0:T(1024)(128)(2,1)S(1)}, bf16[1024]{0:T(1024)(128)(2,1)}, u32[]{:S(2)}) copy-start(bf16[1024]{0:T(1024)(128)(2,1)} %param.29) | copy-start | bytes 6148
  567.4 12.6 %copy-start.1 = (bf16[1024,1536]{1,0:T(8,128)(2,1)S(1)}, bf16[1024,1536]{1,0:T(8,128)(2,1)}, u32[]{:S(2)}) copy-start(bf16[1024,1536]{1,0:T(8,128)(2,1)} %param.18) | copy-start | bytes 9437188
Sparse Core Ops, SparseCore 0:
  15.6 82.7 all-reduce.4
  225.7 45.6 all-reduce.6
  306.1 192.2 all-reduce.8
  521.4 46.0 all-reduce.10
where the time goes:
time: 587 us
  waiting for transfers between devices  366 us (62%)
  other arithmetic  143 us (24%)
  matrix products  45.6 us (8%)
  between operations  14 us (2%)
  blocking collectives  10 us (2%)
  local copies, waits for them, and re-layouts  8.24 us (1%)
    psum x1, waiting for transfers between devices, local_step(): lax.psum(up_part, 'x').astype(jnp.float32) + b_up.astype(jnp.float32)  192 us
    psum x1, waiting for transfers between devices, local_step(): qkv_sum = lax.psum(qkv_part, 'x')  82.2 us
    unnamed x2, other arithmetic  59.2 us
    dot_general x1, other arithmetic, attend(): jnp.einsum('bhs,bshd->bhd', attn_probs, v_full, preferred_element_type=jn...  46.5 us
    psum x1, waiting for transfers between devices, local_step(): down_sum = lax.psum(down_part, 'y')  46.1 us
    psum x1, waiting for transfers between devices, local_step(): proj_sum = lax.psum(proj_part, 'y')  45.7 us
    dot_general x1, matrix products, local_step(): jnp.einsum('bd,dtf->btf', normed, w_up, preferred_element_type=jnp.float32)  23.7 us
  transfers between devices with their start and end apart: 4, of which 4 were waited for; matrix products, arithmetic and copies ran while one was open for 0% of the time, Pallas kernels for 0%

commit v1 on v0

v1 whole, which is shorter than its diff:
```python
import functools
import math
import jax
import jax.numpy as jnp
from jax import lax
from jax.experimental import pallas as pl
from jax.experimental.pallas import tpu as pltpu
from jax.sharding import PartitionSpec as P

DEEP_ALPHA = math.sqrt(140.0)
LN_EPS = 1e-5
ROPE_BASE = 10000.0
HEAD_CHUNKS = 4
UP_CHUNKS = 4
UP_DEPTH_CUTS = 2
STREAMS = 2
SLOT_BLOCK = 8
RING = 16
AHEAD = 8
LANES = 128
TILE = 8
F32 = jnp.float32
BF16 = jnp.bfloat16


def ring_step(t, total, fetch, store, work):
    slot = lax.rem(t, RING)
    fetch(t, slot, False)
    work(slot)
    store(t, slot, True)
    nxt = t + AHEAD
    nxt_slot = lax.rem(nxt, RING)

    @pl.when(jnp.logical_and(nxt < total, nxt >= RING))
    def _():
        store(nxt - RING, nxt_slot, False)

    @pl.when(nxt < total)
    def _():
        fetch(nxt, nxt_slot, True)


def insert_slots(buf, slot, first_slot, len_ref, new_ref, new_row, lane_start, use):
    head_dim = buf.shape[3]
    new_row = new_row if isinstance(new_row, int) else pl.multiple_of(new_row, head_dim)

    def lanes(lb, carry):
        cols = pl.ds(pl.multiple_of(lb * LANES, LANES), LANES)
        ahead = jnp.broadcast_to((len_ref[:, cols] - first_slot).astype(F32), (TILE, LANES)).astype(BF16)
        new = [new_ref[pl.ds(new_row + t, TILE), cols] for t in range(0, head_dim, TILE)]
        state = lane_start(cols)
        for i in range(SLOT_BLOCK):
            here = ahead == jnp.asarray(i, BF16)
            tiles = []
            for j, t in enumerate(range(0, head_dim, TILE)):
                tile = jnp.where(here, new[j], buf[slot, i, 0, t:t + TILE, cols])
                buf[slot, i, 0, t:t + TILE, cols] = tile
                tiles.append(tile)
            state = use(i, cols, tiles, state)
        return carry

    lax.fori_loop(0, len_ref.shape[1] // LANES, lanes, 0)


def attend_kernel(first_ref, own_ref, recv_ref, cos_ref, sin_ref, len_ref, k_ref, v_ref, *rest):
    k_out, v_out, attn_out, k_new_out, v_new_out, buf, query_s, part_s, prob_s, acc_s, in_sem, out_sem = rest[-12:]
    slots, head_dim, rows = k_ref.shape[0], k_ref.shape[2], k_ref.shape[3]
    half_dim = head_dim // 2
    heads = attn_out.shape[0] // head_dim
    groups = slots // SLOT_BLOCK
    total = heads * 2 * groups
    first_head = first_ref[0]

    def copies(t, slot, inward):
        h = first_head + t // (2 * groups)
        g = lax.rem(t, groups)
        at = (pl.ds(g * SLOT_BLOCK, SLOT_BLOCK), pl.ds(h, 1))
        pair = []
        for src, dst in ((k_ref, k_out), (v_ref, v_out)):
            if inward:
                pair.append(functools.partial(pltpu.make_async_copy, src.at[at], buf.at[slot], in_sem.at[slot]))
            else:
                pair.append(functools.partial(pltpu.make_async_copy, buf.at[slot], dst.at[at], out_sem.at[slot]))
        return pair

    def move(inward):
        def go(t, slot, start):
            k_copy, v_copy = copies(t, slot, inward)
            if not start:
                k_copy().wait()
                return
            is_k = lax.rem(t // groups, 2) == 0
            pl.when(is_k)(lambda: k_copy().start())
            pl.when(jnp.logical_not(is_k))(lambda: v_copy().start())

        return go

    fetch, store = move(True), move(False)
    for t in range(AHEAD):
        fetch(jnp.int32(t), jnp.int32(t), True)

    cos_t, sin_t = cos_ref[...], sin_ref[...]

    def rotate(vec):
        lower, upper = vec[:half_dim], vec[half_dim:]
        return jnp.concatenate([lower * cos_t - upper * sin_t, upper * cos_t + lower * sin_t], axis=0).astype(BF16)

    for h in range(heads):
        base = h * 3 * head_dim

        def piece(i):
            at = slice(base + i * head_dim, base + (i + 1) * head_dim)
            return (own_ref[at, :] + recv_ref[at, :].astype(F32)).astype(BF16)

        query_s[...] = rotate(piece(0).astype(F32)).astype(F32) * (head_dim ** -0.5)
        here = slice(h * head_dim, (h + 1) * head_dim)
        k_new_out[here, :] = rotate(piece(1).astype(F32))
        v_new_out[here, :] = piece(2)

        def k_group(g, carry):
            t = h * 2 * groups + g

            def use(i, cols, tiles, query):
                total_p = tiles[0].astype(F32) * query[0]
                for tile, q in zip(tiles[1:], query[1:]):
                    total_p = total_p + tile.astype(F32) * q
                part_s[g * SLOT_BLOCK + i, :, cols] = total_p
                return query

            def load_query(cols):
                return [query_s[d:d + TILE, cols] for d in range(0, head_dim, TILE)]

            ring_step(t, total, fetch, store, lambda slot: insert_slots(buf, slot, g * SLOT_BLOCK, len_ref, k_new_out, h * head_dim, load_query, use))
            return carry

        lax.fori_loop(0, groups, k_group, 0)

        def soft(lb, carry):
            cols = pl.ds(pl.multiple_of(lb * LANES, LANES), LANES)
            slot_ids = lax.broadcasted_iota(jnp.int32, (slots, LANES), 0)
            scores = jnp.sum(part_s[:, :, cols], axis=1)
            scores = jnp.where(slot_ids <= len_ref[:, cols], scores, -1e30)
            expd = jnp.exp(scores - jnp.max(scores, axis=0, keepdims=True))
            prob_s[:, cols] = (expd / jnp.sum(expd, axis=0, keepdims=True)).astype(BF16).astype(F32)
            acc_s[:, cols] = jnp.zeros((head_dim, LANES), F32)
            return carry

        lax.fori_loop(0, rows // LANES, soft, 0)

        def v_group(g, carry):
            t = h * 2 * groups + groups + g

            def load_acc(cols):
                probs = prob_s[pl.ds(pl.multiple_of(g * SLOT_BLOCK, SLOT_BLOCK), SLOT_BLOCK), cols]
                return probs, [acc_s[d:d + TILE, cols] for d in range(0, head_dim, TILE)]

            def use(i, cols, tiles, state):
                probs, acc = state
                prob = jnp.broadcast_to(probs[i:i + 1, :], (TILE, LANES))
                acc = [a + tile.astype(F32) * prob for a, tile in zip(acc, tiles)]
                if i == SLOT_BLOCK - 1:
                    for a, d in zip(acc, range(0, head_dim, TILE)):
                        acc_s[d:d + TILE, cols] = a
                return probs, acc

            ring_step(t, total, fetch, store, lambda slot: insert_slots(buf, slot, g * SLOT_BLOCK, len_ref, v_new_out, h * head_dim, load_acc, use))
            return carry

        lax.fori_loop(0, groups, v_group, 0)
        attn_out[here, :] = acc_s[...].astype(BF16)

    for t in range(max(total - RING, 0), total):
        store(jnp.int32(t), jnp.int32(t % RING), False)


def attend_chunk(first, heads, own, recv, cos_t, sin_t, len_row, k_cache, v_cache, k_prev, v_prev):
    slots, _, head_dim, rows = k_cache.shape
    args = [first, own, recv, cos_t, sin_t, len_row, k_cache, v_cache]
    vmem, hbm = pl.BlockSpec(memory_space=pltpu.VMEM), pl.BlockSpec(memory_space=pl.ANY)
    in_specs = [pl.BlockSpec(memory_space=pltpu.SMEM)] + [vmem] * 5 + [hbm] * 2
    aliases = {}
    if k_prev is not None:
        args += [k_prev, v_prev]
        in_specs += [hbm] * 2
        aliases = {8: 0, 9: 1}
    vec = jax.ShapeDtypeStruct((heads * head_dim, rows), BF16)
    return pl.pallas_call(
        attend_kernel,
        in_specs=in_specs,
        out_specs=[hbm, hbm, vmem, vmem, vmem],
        scratch_shapes=[pltpu.VMEM((RING, SLOT_BLOCK, 1, head_dim, rows), BF16), pltpu.VMEM((head_dim, rows), F32), pltpu.VMEM((slots, 8, rows), F32), pltpu.VMEM((slots, rows), F32), pltpu.VMEM((head_dim, rows), F32), pltpu.SemaphoreType.DMA((RING,)), pltpu.SemaphoreType.DMA((RING,))],
        out_shape=[jax.ShapeDtypeStruct(k_cache.shape, BF16), jax.ShapeDtypeStruct(v_cache.shape, BF16), vec, vec, vec],
        input_output_aliases=aliases,
        compiler_params=pltpu.CompilerParams(vmem_limit_bytes=40 * 2 ** 20),
        cost_estimate=pl.CostEstimate(flops=12_000_000_000 * heads, bytes_accessed=8 * heads * slots * head_dim * rows, transcendentals=0),
    )(*args)


def insert_kernel(first_ref, len_ref, new_ref, c_ref, prev_ref, c_out, buf, in_sem, out_sem):
    slots, head_dim = c_ref.shape[0], c_ref.shape[2]
    heads = new_ref.shape[0] // head_dim
    groups = slots // SLOT_BLOCK
    total = heads * groups
    first_head = first_ref[0]

    def move(inward):
        def go(t, slot, start):
            at = (pl.ds(lax.rem(t, groups) * SLOT_BLOCK, SLOT_BLOCK), pl.ds(first_head + t // groups, 1))
            if inward:
                copy = pltpu.make_async_copy(c_ref.at[at], buf.at[slot], in_sem.at[slot])
            else:
                copy = pltpu.make_async_copy(buf.at[slot], c_out.at[at], out_sem.at[slot])
            copy.start() if start else copy.wait()

        return go

    fetch, store = move(True), move(False)
    for t in range(AHEAD):
        fetch(jnp.int32(t), jnp.int32(t), True)

    def step(t, carry):
        h, g = t // groups, lax.rem(t, groups)
        row = pl.multiple_of(h * head_dim, head_dim)
        ring_step(t, total, fetch, store, lambda slot: insert_slots(buf, slot, g * SLOT_BLOCK, len_ref, new_ref, row, lambda cols: None, lambda i, cols, tiles, state: None))
        return carry

    lax.fori_loop(0, total, step, 0)
    for t in range(max(total - RING, 0), total):
        store(jnp.int32(t), jnp.int32(t % RING), False)


def insert_other(first, len_row, new, cache, prev):
    slots, _, head_dim, rows = cache.shape
    vmem, hbm = pl.BlockSpec(memory_space=pltpu.VMEM), pl.BlockSpec(memory_space=pl.ANY)
    return pl.pallas_call(
        insert_kernel,
        in_specs=[pl.BlockSpec(memory_space=pltpu.SMEM), vmem, vmem, hbm, hbm],
        out_specs=hbm,
        scratch_shapes=[pltpu.VMEM((RING, SLOT_BLOCK, 1, head_dim, rows), BF16), pltpu.SemaphoreType.DMA((RING,)), pltpu.SemaphoreType.DMA((RING,))],
        out_shape=jax.ShapeDtypeStruct(cache.shape, BF16),
        input_output_aliases={4: 0},
        compiler_params=pltpu.CompilerParams(vmem_limit_bytes=24 * 2 ** 20),
        cost_estimate=pl.CostEstimate(flops=5_000_000_000 * (new.shape[0] // head_dim), bytes_accessed=4 * slots * new.shape[0] * rows, transcendentals=0),
    )(first, len_row, new, cache, prev)


def relayout_kernel(block_ref, w_ref, *outs):
    step = pl.program_id(0)
    both = jnp.swapaxes(w_ref[...], 0, 1)
    width = outs[0].shape[2]
    per_cut = pl.num_programs(0) // UP_DEPTH_CUTS
    for i, out in enumerate(outs):
        f, cut = (i // UP_DEPTH_CUTS, i % UP_DEPTH_CUTS) if len(outs) > 1 else (0, None)

        def write(out=out, f=f):
            out[...] = both[:, :, f * width:(f + 1) * width]

        if cut is None:
            write()
        else:
            pl.when(step // per_cut == cut)(write)


def relayout_up(block, w_up, split):
    depth = w_up.shape[0]
    width = w_up.shape[2] // 2
    db = 128
    steps = depth // db
    per_cut = steps // UP_DEPTH_CUTS
    if split:
        fc = width // UP_CHUNKS
        outs = [jax.ShapeDtypeStruct((2, depth // UP_DEPTH_CUTS, fc), BF16)] * (UP_CHUNKS * UP_DEPTH_CUTS)
        specs = [pl.BlockSpec((2, db, fc), lambda d, s, cut=i % UP_DEPTH_CUTS: (0, jnp.clip(d - cut * per_cut, 0, per_cut - 1), 0)) for i in range(len(outs))]
    else:
        outs = [jax.ShapeDtypeStruct((2, depth, width), BF16)]
        specs = [pl.BlockSpec((2, db, width), lambda d, s: (0, d, 0))]
    return pl.pallas_call(
        relayout_kernel,
        grid_spec=pltpu.PrefetchScalarGridSpec(
            num_scalar_prefetch=1, grid=(steps,),
            in_specs=[pl.BlockSpec((db, 2, width), lambda d, s: (d, 0, s[0]))],
            out_specs=specs),
        out_shape=outs,
        compiler_params=pltpu.CompilerParams(vmem_limit_bytes=40 * 2 ** 20),
        cost_estimate=pl.CostEstimate(flops=2_000_000_000, bytes_accessed=8 * depth * width, transcendentals=0),
    )(block, w_up)


def up_kernel(side_ref, za_ref, zo_ref, wa_ref, *rest):
    recv, (b_ref, g_ref) = rest[:-2], rest[-2:]
    cut = recv[0].shape[1]

    def part(t):
        acc = jnp.dot(za_ref[...], wa_ref[t], preferred_element_type=F32)
        for i, w_ref in enumerate(recv):
            acc = acc + jnp.dot(zo_ref[:, i * cut:(i + 1) * cut], w_ref[t], preferred_element_type=F32)
        return acc + b_ref[t:t + 1, :].astype(F32)

    g_ref[...] = (jax.nn.gelu(part(0), approximate=True) * part(1)).astype(BF16)


def up_gated(side, z_own, z_oth, w_all, w_recv, bias, chunk):
    rows, depth = z_own.shape
    width = w_recv[0].shape[2]
    row_block = rows // 2
    z_spec = pl.BlockSpec((row_block, depth), lambda r, s: (r, 0))
    return pl.pallas_call(
        up_kernel,
        grid_spec=pltpu.PrefetchScalarGridSpec(
            num_scalar_prefetch=1, grid=(2,),
            in_specs=[z_spec, z_spec, pl.BlockSpec((2, depth, width), lambda r, s: (0, 0, chunk))] + [pl.BlockSpec(w.shape, lambda r, s: (0, 0, 0)) for w in w_recv] + [pl.BlockSpec((2, width), lambda r, s: (0, chunk))],
            out_specs=pl.BlockSpec((row_block, width), lambda r, s: (r, 0))),
        out_shape=jax.ShapeDtypeStruct((rows, width), BF16),
        compiler_params=pltpu.CompilerParams(vmem_limit_bytes=40 * 2 ** 20),
        cost_estimate=pl.CostEstimate(flops=8 * rows * depth * width, bytes_accessed=8 * depth * width + 4 * rows * depth + 2 * rows * width, transcendentals=rows * width),
        name="upgate",
    )(side, z_own, z_oth, w_all, *w_recv, bias)


def qkv_kernel(block_ref, w_ref, h_ref, b_ref, *outs):
    prod = lax.dot_general(w_ref[...], h_ref[...], (((0,), (1,)), ((), ())), preferred_element_type=F32)
    if outs[0].dtype == F32:
        prod = prod + b_ref[...]
    each = outs[0].shape[0]
    for i, out in enumerate(outs):
        out[...] = prod[i * each:(i + 1) * each].astype(out.dtype)


def qkv_heads(block, w_qkv, hidden, bias, pieces, dtype):
    rows, depth = hidden.shape
    cols = w_qkv.shape[1] // 2
    row_block = rows // 4
    out = jax.ShapeDtypeStruct((cols // pieces, rows), dtype)
    return pl.pallas_call(
        qkv_kernel,
        grid_spec=pltpu.PrefetchScalarGridSpec(
            num_scalar_prefetch=1, grid=(rows // row_block,),
            in_specs=[pl.BlockSpec((depth, cols), lambda r, s: (0, s[0])), pl.BlockSpec((row_block, depth), lambda r, s: (r, 0)), pl.BlockSpec((cols, 1), lambda r, s: (s[0], 0))],
            out_specs=[pl.BlockSpec((cols // pieces, row_block), lambda r, s: (0, r))] * pieces),
        out_shape=[out] * pieces,
        compiler_params=pltpu.CompilerParams(vmem_limit_bytes=60 * 2 ** 20),
        cost_estimate=pl.CostEstimate(flops=2 * rows * depth * cols, bytes_accessed=2 * depth * (rows + cols) + 4 * rows * cols, transcendentals=0),
    )(block, w_qkv, hidden, bias)


def solution(mesh):
    cache_spec = P('dp', None, 'y', None)
    width_spec = P('x')
    in_specs = (P('dp', 'x'), P('x', 'y'), P('y'), P('y', 'x'), width_spec, width_spec, width_spec, P('x', None, 'y'), P(None, 'y'), P('y', 'x'), width_spec, width_spec, width_spec, cache_spec, cache_spec, P('dp'), P('dp'))
    out_specs = (P('dp', 'x'), cache_spec, cache_spec)
    swap_x = [(0, 1), (1, 0)]
    swap_core = [(i, i ^ 1) for i in range(4)]
    swap_chip = [(i, i ^ 2) for i in range(4)]

    def over_x(v):
        return lax.ppermute(v, 'x', swap_x)

    def over_core(v):
        return lax.ppermute(v, 'y', swap_core)

    def over_chip(v):
        return lax.ppermute(v, 'y', swap_chip)

    def layer(hidden, w_qkv, b_qkv, w_out, b_out, attn_gain, attn_shift, w_up, b_up, w_down, b_down, mlp_gain, mlp_shift, k_cache, v_cache, positions, lengths):
        rows, width = hidden.shape
        width_all = 2 * width
        _, local_heads, head_dim = k_cache.shape[1:]
        half_heads = local_heads // 2
        heads_c = half_heads // HEAD_CHUNKS
        side = lax.axis_index('x')
        y_index = lax.axis_index('y')
        side_arr = side[None].astype(jnp.int32)
        own_first = [side * half_heads + j * heads_c for j in range(HEAD_CHUNKS)]
        oth_first = [(1 - side) * half_heads + j * heads_c for j in range(HEAD_CHUNKS)]
        bias_col = b_qkv.astype(F32)[:, None]
        qkv_send = qkv_heads((1 - side)[None].astype(jnp.int32), w_qkv, hidden, bias_col, HEAD_CHUNKS, BF16)
        qkv_recv = [over_x(v) for v in qkv_send]
        hidden_late, _ = lax.optimization_barrier((hidden, qkv_send[0]))
        qkv_own = qkv_heads(side_arr, w_qkv, hidden_late, bias_col, HEAD_CHUNKS, F32)

        len_row = lengths[None]
        inv_freq = ROPE_BASE ** (-2.0 * jnp.arange(head_dim // 2, dtype=F32) / head_dim)
        angles = inv_freq[:, None] * positions.astype(F32)[None, :]
        cos_t, sin_t = jnp.cos(angles), jnp.sin(angles)

        f_half = w_up.shape[2] // 2
        w_down_own = lax.dynamic_slice_in_dim(w_down, side * f_half, f_half, 0)
        w_down_oth = lax.dynamic_slice_in_dim(w_down, (1 - side) * f_half, f_half, 0)
        w_out_own = lax.dynamic_slice_in_dim(w_out, side * half_heads * head_dim, half_heads * head_dim, 0)
        w_out_oth = lax.dynamic_slice_in_dim(w_out, (1 - side) * half_heads * head_dim, half_heads * head_dim, 0)

        w_up_early, _ = lax.optimization_barrier((w_up, qkv_own[0]))
        w_up_send = relayout_up((1 - side)[None].astype(jnp.int32), w_up_early, True)
        w_up_recv = [[over_x(w_up_send[i * UP_DEPTH_CUTS + d]) for d in range(UP_DEPTH_CUTS)] for i in range(UP_CHUNKS)]

        k_t = jnp.transpose(k_cache, (1, 2, 3, 0))
        v_t = jnp.transpose(v_cache, (1, 2, 3, 0))
        k_full = v_full = None
        attn_own, attn_recv, k_new, v_new = [], [], [], []
        for j in range(HEAD_CHUNKS):
            k_full, v_full, attn_c, k_c, v_c = attend_chunk(own_first[j][None].astype(jnp.int32), heads_c, qkv_own[j], qkv_recv[j], cos_t, sin_t, len_row, k_t, v_t, k_full, v_full)
            attn_own.append(attn_c)
            attn_recv.append(over_x(attn_c))
            k_new.append(k_c)
            v_new.append(v_c)
        attn_own = jnp.concatenate(attn_own, axis=0)
        attn_recv = jnp.concatenate(attn_recv, axis=0)
        w_up_late, _ = lax.optimization_barrier((w_up, attn_own))
        w_up_t, = relayout_up(side_arr, w_up_late, False)
        b_up_own = lax.dynamic_slice_in_dim(b_up, side * f_half, f_half, 1)

        quarter = rows // 4
        piece = quarter // STREAMS
        hid_q = lax.dynamic_slice_in_dim(hidden, y_index * quarter, quarter, 0)
        near = (0, 2, 1, 3)

        def reduce_scatter_y(part):
            two = part[:2 * piece].astype(F32) + over_core(part[2 * piece:].astype(BF16)).astype(F32)
            return two[:piece] + over_chip(two[piece:].astype(BF16)).astype(F32)

        def gather_y(val):
            both = jnp.concatenate([val, over_chip(val)], axis=0)
            return jnp.concatenate([both, over_core(both)], axis=0)

        def norm(h_val, gain, shift):
            mean_l = jnp.mean(h_val, axis=1)
            dev = jnp.sum(jnp.square(h_val - mean_l[:, None]), axis=1)
            other = over_x(jnp.stack([mean_l, dev]))
            mean_row = 0.5 * (mean_l + other[0])
            var_row = (dev + other[1] + (width / 2) * jnp.square(mean_l - other[0])) / width_all
            scaled = (h_val - mean_row[:, None]) * lax.rsqrt(var_row + LN_EPS)[:, None]
            return (scaled * gain.astype(F32) + shift.astype(F32)).astype(BF16)

        k_recv = over_x(jnp.concatenate(k_new, axis=0))
        v_recv = over_x(jnp.concatenate(v_new, axis=0))
        outs = []
        for r in range(STREAMS):
            starts = [(y_index ^ i) * quarter + r * piece for i in near]

            def project(attn_t, w):
                rel = jnp.concatenate([lax.dynamic_slice_in_dim(attn_t, s, piece, 1) for s in starts], axis=1)
                return lax.dot_general(rel, w, (((0,), (0,)), ((), ())), preferred_element_type=F32)

            part = project(attn_own, w_out_own)
            proj_sum = reduce_scatter_y(part + project(attn_recv, w_out_oth))
            h_attn = DEEP_ALPHA * hid_q[r * piece:(r + 1) * piece].astype(F32) + proj_sum + b_out.astype(F32)
            z_q = norm(h_attn, attn_gain, attn_shift)
            z_own = gather_y(z_q)
            z_oth = gather_y(over_x(z_q))
            g_own, g_recv = [], []
            for i in range(UP_CHUNKS):
                g_own.append(up_gated(side_arr, z_own, z_oth, w_up_t, w_up_recv[i], b_up_own, i))
                g_recv.append(over_x(g_own[-1]))
            down = jnp.dot(jnp.concatenate(g_own, axis=1), w_down_own, preferred_element_type=F32)
            down = down + jnp.dot(jnp.concatenate(g_recv, axis=1), w_down_oth, preferred_element_type=F32)
            down_sum = reduce_scatter_y(down)
            h_mlp = DEEP_ALPHA * z_q.astype(F32) + down_sum + b_down.astype(F32)
            outs.append(gather_y(norm(h_mlp, mlp_gain, mlp_shift)).reshape(4, piece, width))
        result = jnp.stack(outs, axis=1)
        order = [jnp.where((y_index ^ j) == 1, 2, jnp.where((y_index ^ j) == 2, 1, y_index ^ j)) for j in range(4)]
        result = jnp.concatenate([lax.dynamic_index_in_dim(result, o, 0, keepdims=False).reshape(quarter, width) for o in order], axis=0)

        cut = half_heads * head_dim // 2
        for i in range(2):
            first = (oth_first[0] + i * half_heads // 2)[None].astype(jnp.int32)
            k_full = insert_other(first, len_row, k_recv[i * cut:(i + 1) * cut], k_t, k_full)
            v_full = insert_other(first, len_row, v_recv[i * cut:(i + 1) * cut], v_t, v_full)
        return result, jnp.transpose(k_full, (3, 0, 1, 2)), jnp.transpose(v_full, (3, 0, 1, 2))

    return jax.shard_map(layer, mesh=mesh, in_specs=in_specs, out_specs=out_specs, check_vma=False)
```

time: 587 us -> 329 us (0.56)
  waiting for transfers between devices: 366 us -> 125 us
  other arithmetic: 143 us -> 10.7 us
  Pallas kernels: 0 us -> 129 us
  starting transfers between devices: 0.16 us -> 40.9 us
  matrix products: 45.6 us -> 6.97 us
  between operations: 14 us -> 1.7 us
  blocking collectives: 10 us -> 0 us
    psum x4 -> x0, waiting for transfers between devices: 366 us -> none  [the longest x1 192 us: local_step(): lax.psum(up_part, 'x').astype(jnp.float32) + b_up.astype(jnp.float32)]
    pallas_call x0 -> x20, Pallas kernels: none -> 129 us  [the longest x4 49.8 us: attend_chunk(): pl.pallas_call(attend_kernel, in_specs=in_specs, out_specs=[hbm, hbm, vme...]
    ppermute x0 -> x52, waiting for transfers between devices: none -> 125 us  [the longest x32 108 us: over_x(): return lax.ppermute(v, 'x', swap_x)]
    unnamed x2 -> x1, other arithmetic: 59.2 us -> 0.01 us
    dot_general x1 -> x0, other arithmetic: 46.5 us -> none  [attend(): jnp.einsum('bhs,bshd->bhd', attn_probs, v_full, preferred_element_type=jn...]
    ppermute x0 -> x52, starting transfers between devices: none -> 40.9 us  [the longest x32 29.7 us: over_x(): return lax.ppermute(v, 'x', swap_x)]
    dot_general x4 -> x8, matrix products: 45.6 us -> 6.97 us  [the longest x2 2.57 us: layer(): jnp.dot(jnp.concatenate(g_own, axis=1), w_down_own, preferred_element_typ...]
    psum x2 -> x0, blocking collectives: 10 us -> none  [sharded_norm(): moments = lax.psum(moments, 'x')]
  transfers between devices with their start and end apart: 4 -> 52, of which waited for: 4 -> 25; matrix products, arithmetic and copies ran while one was open for 0% -> 5% of each run, Pallas kernels for 0% -> 38%
where the time goes in v1:
time: 329 us
  Pallas kernels  129 us (39%)
  waiting for transfers between devices  125 us (38%)
  starting transfers between devices  40.9 us (12%)
  local copies, waits for them, and re-layouts  14 us (4%)
  other arithmetic  10.7 us (3%)
  matrix products  6.97 us (2%)
    ppermute x32, waiting for transfers between devices, over_x(): return lax.ppermute(v, 'x', swap_x)  108 us
    pallas_call x4, Pallas kernels, attend_chunk(): pl.pallas_call(attend_kernel, in_specs=in_specs, out_specs=[hbm, hbm, vme...  49.8 us
    pallas_call x4, Pallas kernels, insert_other(): pl.pallas_call(insert_kernel, in_specs=[pl.BlockSpec(memory_space=pltpu.S...  49.5 us
    ppermute x32, starting transfers between devices, over_x(): return lax.ppermute(v, 'x', swap_x)  29.7 us
    ppermute x10, waiting for transfers between devices, over_chip(): return lax.ppermute(v, 'y', swap_chip)  16.5 us
    pallas_call x8, Pallas kernels, up_gated(): pl.pallas_call(up_kernel, grid_spec=pltpu.PrefetchScalarGridSpec(num_scal...  13.8 us
    pallas_call x2, Pallas kernels, qkv_heads(): pl.pallas_call(qkv_kernel, grid_spec=pltpu.PrefetchScalarGridSpec(num_sca...  10.9 us
    ppermute x10, starting transfers between devices, over_chip(): return lax.ppermute(v, 'y', swap_chip)  10.2 us
  transfers between devices with their start and end apart: 52, of which 25 were waited for; matrix products, arithmetic and copies ran while one was open for 5% of the time, Pallas kernels for 38%

profile of v1, /device:TPU:0, one launch (start us, length us, event | category | flops | bytes accessed | tf_op | source)
XLA Modules:
  0.0 328.8 jit_solution(1185693481641102982)
XLA Ops:
  0.7 1.9 reshape.199.b_ref
  2.6 5.3 %shard_map.184 = (bf16[192,1024]{1,0:T(8,128)(2,1)}, bf16[192,1024]{1,0:T(8,128)(2,1)}, bf16[192,1024]{1,0:T(8,128)(2,1)}, bf16[192,1024]{1,0:T(8,128)(2,1)}) custom-call(s32[1]{0:T(128)} %bitcast.2.block_ref, bf16[1024,1536]{1,0:T(8,128)(2,1)} %w_ref.3, bf16[1024,1024]{1,0:T(8,128)(2,1)} %h_ref.2, f32[1536,1]{1,0:T(8,128)} %reshape.199.b_ref), custom_call_target="tpu_custom_call" | custom-call | flops 1610612736 | bytes 6815744 | tf_op jit(solution)/shard_map/pallas_call | solution.py:334
  7.9 3.3 %collective-permute-start = (bf16[192,1024]{1,0:T(8,128)(2,1)}, bf16[192,1024]{1,0:T(8,128)(2,1)S(1)}, u32[]{:S(2)}, u32[]{:S(2)}) collective-permute-start(bf16[192,1024]{1,0:T(8,128)(2,1)} %get-tuple-element.42), channel_id=1, source_target_pairs={{0,4},{4,0},{1,5},{5,1},{2,6},{6,2},{3,7},{7,3}} | collective-permute-start | bytes 1179656 | tf_op jit(solution)/shard_map/ppermute | solution.py:356
  11.2 2.0 collective-permute-start.2
  13.3 5.6 %shard_map.185 = (f32[192,1024]{1,0:T(8,128)}, f32[192,1024]{1,0:T(8,128)}, f32[192,1024]{1,0:T(8,128)}, f32[192,1024]{1,0:T(8,128)}) custom-call(s32[1]{0:T(128)} %bitcast.1.block_ref.side_ref, bf16[1024,1536]{1,0:T(8,128)(2,1)} %w_ref.3, bf16[1024,1024]{1,0:T(8,128)(2,1)} %h_ref.2, f32[1536,1]{1,0:T(8,128)} %reshape.199.b_ref), custom_call_target="tpu_custom_call" | custom-call | flops 1610612736 | bytes 6815744 | tf_op jit(solution)/shard_map/pallas_call | solution.py:334
  19.5 1.9 collective-permute-done.recv_ref
  22.5 12.2 %shard_map.186 = (bf16[64,8,64,1024]{3,2,1,0:T(8,128)(2,1)}, bf16[64,8,64,1024]{3,2,1,0:T(8,128)(2,1)}, bf16[64,1024]{1,0:T(8,128)(2,1)S(1)}, bf16[64,1024]{1,0:T(8,128)(2,1)S(1)}, bf16[64,1024]{1,0:T(8,128)(2,1)S(1)}) custom-call(s32[1]{0:T(128)} %bitcast.first_ref, f32[192,1024]{1,0:T(8,128)S(1)} %copy-done.6, ...), custom_call_target="tpu_custom_call" | custom-call | flops 12000000000 | bytes 33554432 | tf_op jit(solution)/shard_map/pallas_call | solution.py:187
  34.8 12.2 %shard_map.187 = (bf16[64,8,64,1024]{3,2,1,0:T(8,128)(2,1)}, bf16[64,8,64,1024]{3,2,1,0:T(8,128)(2,1)}, bf16[64,1024]{1,0:T(8,128)(2,1)S(1)}, bf16[64,1024]{1,0:T(8,128)(2,1)S(1)}, bf16[64,1024]{1,0:T(8,128)(2,1)S(1)}) custom-call(s32[1]{0:T(128)} %bitcast.6.first_ref, f32[192,1024]{1,0:T(8,128)S(1)} %copy-done.5, ...), custom_call_target="tpu_custom_call", output_to_operand_aliasing={{0}: (8, {}), {1}: (9, {})} | custom-call | flops 12000000000 | bytes 33554432 | tf_op jit(solution)/shard_map/pallas_call | solution.py:187
  47.1 12.2 %shard_map.188 = (bf16[64,8,64,1024]{3,2,1,0:T(8,128)(2,1)}, bf16[64,8,64,1024]{3,2,1,0:T(8,128)(2,1)}, bf16[64,1024]{1,0:T(8,128)(2,1)S(1)}, bf16[64,1024]{1,0:T(8,128)(2,1)S(1)}, bf16[64,1024]{1,0:T(8,128)(2,1)S(1)}) custom-call(s32[1]{0:T(128)} %bitcast.7.first_ref, f32[192,1024]{1,0:T(8,128)S(1)} %copy-done.4, ...), custom_call_target="tpu_custom_call", output_to_operand_aliasing={{0}: (8, {}), {1}: (9, {})} | custom-call | flops 12000000000 | bytes 33554432 | tf_op jit(solution)/shard_map/pallas_call | solution.py:187
  59.3 2.0 collective-permute-start.6
  61.4 2.0 collective-permute-start.4
  63.4 13.1 %shard_map.189 = (bf16[64,8,64,1024]{3,2,1,0:T(8,128)(2,1)}, bf16[64,8,64,1024]{3,2,1,0:T(8,128)(2,1)}, bf16[64,1024]{1,0:T(8,128)(2,1)S(1)}, bf16[64,1024]{1,0:T(8,128)(2,1)S(1)}, bf16[64,1024]{1,0:T(8,128)(2,1)S(1)}) custom-call(s32[1]{0:T(128)} %bitcast.8.first_ref, f32[192,1024]{1,0:T(8,128)S(1)} %copy-done.3, ...), custom_call_target="tpu_custom_call", output_to_operand_aliasing={{0}: (8, {}), {1}: (9, {})} | custom-call | flops 12000000000 | bytes 33554432 | tf_op jit(solution)/shard_map/pallas_call | solution.py:187
  77.9 3.7 %collective-permute-done.7 = bf16[64,1024]{1,0:T(8,128)(2,1)S(1)} collective-permute-done((bf16[64,1024]{1,0:T(8,128)(2,1)S(1)}, bf16[64,1024]{1,0:T(8,128)(2,1)S(1)}, u32[]{:S(2)}, u32[]{:S(2)}) %collective-permute-start.7) | collective-permute-done | bytes 131104 | tf_op jit(solution)/shard_map/ppermute | solution.py:356
  85.7 3.8 %shard_map.191 = (bf16[2,512,256]{2,1,0:T(8,128)(2,1)}, bf16[2,512,256]{2,1,0:T(8,128)(2,1)}, bf16[2,512,256]{2,1,0:T(8,128)(2,1)S(1)}, bf16[2,512,256]{2,1,0:T(...) custom-call(s32[1]{0:T(128)} %bitcast.2.block_ref, ...), custom_call_target="tpu_custom_call" | custom-call | flops 2000000000 | bytes 8388608 | tf_op jit(solution)/shard_map/pallas_call | solution.py:277
  93.5 2.0 collective-permute-start.17
  97.4 1.5 slice_add_fusion.3
  99.0 1.5 collective-permute-start.9
  102.6 3.4 %copy-done.2 = bf16[1024,2,2048]{2,1,0:T(2,128)(2,1)S(1)} copy-done((bf16[1024,2,2048]{2,1,0:T(2,128)(2,1)S(1)}, bf16[1024,2,2048]{2,1,0:T(2,128)(2,1)}, u32[]{:S(2)}) %copy-start.2) | copy-done | bytes 8388632
  106.0 1.5 shard_map.190.wa_ref
  108.2 4.2 %collective-permute-done.34 = bf16[128,1024]{1,0:T(8,128)(2,1)S(1)} collective-permute-done((bf16[128,1024]{1,0:T(8,128)(2,1)S(1)}, bf16[128,1024]{1,0:T(8,128)(2,1)S(1)}, u32[]{:S(2)}, u32[]{:S(2)}) %collective-permute-start.34) | collective-permute-done | bytes 262176 | tf_op jit(solution)/shard_map/ppermute | solution.py:362
  112.4 1.4 fusion.130
  114.4 1.7 collective-permute-start.35
  116.1 14.1 %collective-permute-done.10 = f32[2,128]{1,0:T(2,128)S(1)} collective-permute-done((f32[2,128]{1,0:T(2,128)S(1)}, f32[2,128]{1,0:T(2,128)S(1)}, u32[]{:S(2)}, u32[]{:S(2)}) %collective-permute-start.10) | collective-permute-done | bytes 1056 | tf_op jit(solution)/shard_map/ppermute | solution.py:356
  130.5 1.5 collective-permute-start.11
  132.6 1.5 collective-permute-start.38
  134.2 3.8 %collective-permute-done.11 = bf16[128,1024]{1,0:T(8,128)(2,1)S(1)} collective-permute-done((bf16[128,1024]{1,0:T(8,128)(2,1)S(1)}, bf16[128,1024]{1,0:T(8,128)(2,1)S(1)}, u32[]{:S(2)}, u32[]{:S(2)}) %collective-permute-start.11) | collective-permute-done | bytes 262176 | tf_op jit(solution)/shard_map/ppermute | solution.py:362
  138.0 1.5 collective-permute-start.36
  139.4 12.4 %shard_map.194.prev_ref = bf16[64,8,64,1024]{3,2,1,0:T(8,128)(2,1)} custom-call(s32[1]{0:T(128)} %bitcast.32.first_ref, s32[1,1024]{1,0:T(1,128)S(1)} %bitcast.121, bf16[128,1024]{1,0:T(8,128)(2,1)S(1)} %get-tuple-element.95.new_ref, bf16[64,8,64,1024]{3,2,1,0:T(8,128)(2,1)} %bitcast.5.v_ref.c_ref, ...), custom_call_target="tpu_custom_call", output_to_operand_aliasing={{}: (4, {})} | custom-call | flops 10000000000 | bytes 33554432 | tf_op jit(solution)/shard_map/pallas_call | solution.py:235
  153.1 1.4 collective-permute-start.39
  154.7 1.5 collective-permute-start.19
  156.2 5.1 %collective-permute-done.14 = bf16[128,1024]{1,0:T(8,128)(2,1)S(1)} collective-permute-done((bf16[128,1024]{1,0:T(8,128)(2,1)S(1)}, bf16[128,1024]{1,0:T(8,128)(2,1)S(1)}, u32[]{:S(2)}, u32[]{:S(2)}) %collective-permute-start.14) | collective-permute-done | bytes 262176 | tf_op jit(solution)/shard_map/ppermute | solution.py:362
  161.3 2.8 collective-permute-done.39
  164.2 2.6 collective-permute-done.18.rest_0_
  167.3 1.5 collective-permute-start.21
  168.9 9.1 %collective-permute-done.19.rest_1_ = bf16[2,512,256]{2,1,0:T(8,128)(2,1)S(1)} collective-permute-done((bf16[2,512,256]{2,1,0:T(8,128)(2,1)S(1)}, bf16[2,512,256]{2,1,0:T(8,128)(2,1)S(1)}, u32[]{:S(2)}, u32[]{:S(2)}) %collective-permute-start.19) | collective-permute-done | bytes 524320 | tf_op jit(solution)/shard_map/ppermute | solution.py:356
  178.5 1.5 collective-permute-start.23
  180.2 1.7 upgate.8
  181.9 1.7 upgate.9
  183.7 5.6 %collective-permute-done.20.rest_0_ = bf16[2,512,256]{2,1,0:T(8,128)(2,1)S(1)} collective-permute-done((bf16[2,512,256]{2,1,0:T(8,128)(2,1)S(1)}, bf16[2,512,256]{2,1,0:T(8,128)(2,1)S(1)}, u32[]{:S(2)}, u32[]{:S(2)}) %collective-permute-start.20) | collective-permute-done | bytes 524320 | tf_op jit(solution)/shard_map/ppermute | solution.py:356
  189.7 10.7 %collective-permute-done.21.rest_1_ = bf16[2,512,256]{2,1,0:T(8,128)(2,1)S(1)} collective-permute-done((bf16[2,512,256]{2,1,0:T(8,128)(2,1)S(1)}, bf16[2,512,256]{2,1,0:T(8,128)(2,1)S(1)}, u32[]{:S(2)}, u32[]{:S(2)}) %collective-permute-start.21) | collective-permute-done | bytes 524320 | tf_op jit(solution)/shard_map/ppermute | solution.py:356
  201.0 1.7 upgate.10
  202.7 9.0 %collective-permute-done.22.rest_0_ = bf16[2,512,256]{2,1,0:T(8,128)(2,1)S(1)} collective-permute-done((bf16[2,512,256]{2,1,0:T(8,128)(2,1)S(1)}, bf16[2,512,256]{2,1,0:T(8,128)(2,1)S(1)}, u32[]{:S(2)}, u32[]{:S(2)}) %collective-permute-start.22) | collective-permute-done | bytes 524320 | tf_op jit(solution)/shard_map/ppermute | solution.py:356
  212.2 10.7 %collective-permute-done.23.rest_1_ = bf16[2,512,256]{2,1,0:T(8,128)(2,1)S(1)} collective-permute-done((bf16[2,512,256]{2,1,0:T(8,128)(2,1)S(1)}, bf16[2,512,256]{2,1,0:T(8,128)(2,1)S(1)}, u32[]{:S(2)}, u32[]{:S(2)}) %collective-permute-start.23) | collective-permute-done | bytes 524320 | tf_op jit(solution)/shard_map/ppermute | solution.py:356
  223.4 1.7 upgate.11
  225.2 1.5 collective-permute-start.27
  226.7 1.7 upgate.12
  228.5 1.7 upgate.13
  230.2 1.7 upgate.14
  232.0 1.7 upgate.15
  233.7 6.1 %collective-permute-done.24 = bf16[512,256]{1,0:T(8,128)(2,1)S(1)} collective-permute-done((bf16[512,256]{1,0:T(8,128)(2,1)S(1)}, bf16[512,256]{1,0:T(8,128)(2,1)S(1)}, u32[]{:S(2)}, u32[]{:S(2)}) %collective-permute-start.24) | collective-permute-done | bytes 262176 | tf_op jit(solution)/shard_map/ppermute | solution.py:356
  240.3 5.1 %collective-permute-done.25 = bf16[512,256]{1,0:T(8,128)(2,1)S(1)} collective-permute-done((bf16[512,256]{1,0:T(8,128)(2,1)S(1)}, bf16[512,256]{1,0:T(8,128)(2,1)S(1)}, u32[]{:S(2)}, u32[]{:S(2)}) %collective-permute-start.25) | collective-permute-done | bytes 262176 | tf_op jit(solution)/shard_map/ppermute | solution.py:356
  245.9 5.1 %collective-permute-done.26 = bf16[512,256]{1,0:T(8,128)(2,1)S(1)} collective-permute-done((bf16[512,256]{1,0:T(8,128)(2,1)S(1)}, bf16[512,256]{1,0:T(8,128)(2,1)S(1)}, u32[]{:S(2)}, u32[]{:S(2)}) %collective-permute-start.26) | collective-permute-done | bytes 262176 | tf_op jit(solution)/shard_map/ppermute | solution.py:356
  251.5 5.1 %collective-permute-done.27 = bf16[512,256]{1,0:T(8,128)(2,1)S(1)} collective-permute-done((bf16[512,256]{1,0:T(8,128)(2,1)S(1)}, bf16[512,256]{1,0:T(8,128)(2,1)S(1)}, u32[]{:S(2)}, u32[]{:S(2)}) %collective-permute-start.27) | collective-permute-done | bytes 262176 | tf_op jit(solution)/shard_map/ppermute | solution.py:356
  258.4 1.3 fusion.8
  259.8 2.5 collective-permute-done.41
  262.3 5.6 %collective-permute-done.42 = bf16[512,256]{1,0:T(8,128)(2,1)S(1)} collective-permute-done((bf16[512,256]{1,0:T(8,128)(2,1)S(1)}, bf16[512,256]{1,0:T(8,128)(2,1)S(1)}, u32[]{:S(2)}, u32[]{:S(2)}) %collective-permute-start.42) | collective-permute-done | bytes 262176 | tf_op jit(solution)/shard_map/ppermute | solution.py:356
  267.9 5.5 %collective-permute-done.43 = bf16[512,256]{1,0:T(8,128)(2,1)S(1)} collective-permute-done((bf16[512,256]{1,0:T(8,128)(2,1)S(1)}, bf16[512,256]{1,0:T(8,128)(2,1)S(1)}, u32[]{:S(2)}, u32[]{:S(2)}) %collective-permute-start.43) | collective-permute-done | bytes 262176 | tf_op jit(solution)/shard_map/ppermute | solution.py:356
  273.4 2.8 collective-permute-done.44
  277.5 1.3 fusion.11
  281.6 12.4 %shard_map.192.prev_ref = bf16[64,8,64,1024]{3,2,1,0:T(8,128)(2,1)} custom-call(s32[1]{0:T(128)} %bitcast.32.first_ref, s32[1,1024]{1,0:T(1,128)S(1)} %bitcast.122, bf16[128,1024]{1,0:T(8,128)(2,1)S(1)} %get-tuple-element.97.new_ref, bf16[64,8,64,1024]{3,2,1,0:T(8,128)(2,1)} %bitcast.4.k_ref.c_ref, ...), custom_call_target="tpu_custom_call", output_to_operand_aliasing={{}: (4, {})} | custom-call | flops 10000000000 | bytes 33554432 | tf_op jit(solution)/shard_map/pallas_call | solution.py:235
  296.8 1.3 collective-permute-done.30
  301.5 12.4 %shard_map.195 = bf16[64,8,64,1024]{3,2,1,0:T(8,128)(2,1)} custom-call(s32[1]{0:T(128)} %bitcast.31.first_ref, s32[1,1024]{1,0:T(1,128)S(1)} %bitcast.123, bf16[128,1024]{1,0:T(8,128)(2,1)S(1)} %get-tuple-element.96.new_ref, bf16[64,8,64,1024]{3,2,1,0:T(8,128)(2,1)} %bitcast.5.v_ref.c_ref, ...), custom_call_target="tpu_custom_call", output_to_operand_aliasing={{}: (4, {})} | custom-call | flops 10000000000 | bytes 33554432 | tf_op jit(solution)/shard_map/pallas_call | solution.py:235
  314.6 12.4 %shard_map.193 = bf16[64,8,64,1024]{3,2,1,0:T(8,128)(2,1)} custom-call(s32[1]{0:T(128)} %bitcast.31.first_ref, s32[1,1024]{1,0:T(1,128)S(1)} %bitcast.124, bf16[128,1024]{1,0:T(8,128)(2,1)S(1)} %get-tuple-element.98.new_ref, bf16[64,8,64,1024]{3,2,1,0:T(8,128)(2,1)} %bitcast.4.k_ref.c_ref, ...), custom_call_target="tpu_custom_call", output_to_operand_aliasing={{}: (4, {})} | custom-call | flops 10000000000 | bytes 33554432 | tf_op jit(solution)/shard_map/pallas_call | solution.py:235
  327.3 1.5 pad_maximum_fusion
  (213 shorter events, 36.4 us)
Async XLA Ops:
  0.6 76.2 %copy-start = (bf16[512,1024]{1,0:T(8,128)(2,1)S(1)}, bf16[512,1024]{1,0:T(8,128)(2,1)}, u32[]{:S(2)}) copy-start(bf16[512,1024]{1,0:T(8,128)(2,1)} %param.20) | copy-start | bytes 3145732
  7.9 13.5 %collective-permute-start = (bf16[192,1024]{1,0:T(8,128)(2,1)}, bf16[192,1024]{1,0:T(8,128)(2,1)S(1)}, u32[]{:S(2)}, u32[]{:S(2)}) collective-permute-start(bf16[192,1024]{1,0:T(8,128)(2,1)} %get-tuple-element.42), channel_id=1, source_target_pairs={{0,4},{4,0},{1,5},{5,1},{2,6},{6,2},{3,7},{7,3}} | collective-permute-start | bytes 1179656 | tf_op jit(solution)/shard_map/ppermute | solution.py:356
  11.2 23.6 %collective-permute-start.1 = (bf16[192,1024]{1,0:T(8,128)(2,1)}, bf16[192,1024]{1,0:T(8,128)(2,1)S(1)}, u32[]{:S(2)}, u32[]{:S(2)}) collective-permute-start(bf16[192,1024]{1,0:T(8,128)(2,1)} %get-tuple-element.47), channel_id=1, source_target_pairs={{0,4},{4,0},{1,5},{5,1},{2,6},{6,2},{3,7},{7,3}} | collective-permute-start | bytes 1179656 | tf_op jit(solution)/shard_map/ppermute | solution.py:356
  11.2 35.8 %collective-permute-start.2 = (bf16[192,1024]{1,0:T(8,128)(2,1)}, bf16[192,1024]{1,0:T(8,128)(2,1)S(1)}, u32[]{:S(2)}, u32[]{:S(2)}) collective-permute-start(bf16[192,1024]{1,0:T(8,128)(2,1)} %get-tuple-element.52), channel_id=1, source_target_pairs={{0,4},{4,0},{1,5},{5,1},{2,6},{6,2},{3,7},{7,3}} | collective-permute-start | bytes 1179656 | tf_op jit(solution)/shard_map/ppermute | solution.py:356
  13.2 50.2 %collective-permute-start.3 = (bf16[192,1024]{1,0:T(8,128)(2,1)}, bf16[192,1024]{1,0:T(8,128)(2,1)}, u32[]{:S(2)}, u32[]{:S(2)}) collective-permute-start(bf16[192,1024]{1,0:T(8,128)(2,1)} %get-tuple-element.57), channel_id=1, source_target_pairs={{0,4},{4,0},{1,5},{5,1},{2,6},{6,2},{3,7},{7,3}} | collective-permute-start | bytes 1179656 | tf_op jit(solution)/shard_map/ppermute | solution.py:356
  22.5 12.2 %copy-start.5 = (f32[192,1024]{1,0:T(8,128)S(1)}, f32[192,1024]{1,0:T(8,128)}, u32[]{:S(2)}) copy-start(f32[192,1024]{1,0:T(8,128)} %get-tuple-element.46.own_ref) | copy-start | bytes 2359300
  34.8 12.3 %copy-start.4 = (f32[192,1024]{1,0:T(8,128)S(1)}, f32[192,1024]{1,0:T(8,128)}, u32[]{:S(2)}) copy-start(f32[192,1024]{1,0:T(8,128)} %get-tuple-element.51.own_ref) | copy-start | bytes 2359300
  47.0 16.4 %copy-start.3 = (f32[192,1024]{1,0:T(8,128)S(1)}, f32[192,1024]{1,0:T(8,128)}, u32[]{:S(2)}) copy-start(f32[192,1024]{1,0:T(8,128)} %get-tuple-element.56.own_ref) | copy-start | bytes 2359300
  59.3 18.5 %collective-permute-start.6 = (bf16[64,1024]{1,0:T(8,128)(2,1)S(1)}, bf16[64,1024]{1,0:T(8,128)(2,1)S(1)}, u32[]{:S(2)}, u32[]{:S(2)}) collective-permute-start(bf16[64,1024]{1,0:T(8,128)(2,1)S(1)} %get-tuple-element.55), channel_id=1, source_target_pairs={{0,4},{4,0},{1,5},{5,1},{2,6},{6,2},{3,7},{7,3}} | collective-permute-start | bytes 393224 | tf_op jit(solution)/shard_map/ppermute | solution.py:356
  61.3 16.5 %collective-permute-start.5 = (bf16[64,1024]{1,0:T(8,128)(2,1)S(1)}, bf16[64,1024]{1,0:T(8,128)(2,1)S(1)}, u32[]{:S(2)}, u32[]{:S(2)}) collective-permute-start(bf16[64,1024]{1,0:T(8,128)(2,1)S(1)} %get-tuple-element.50), channel_id=1, source_target_pairs={{0,4},{4,0},{1,5},{5,1},{2,6},{6,2},{3,7},{7,3}} | collective-permute-start | bytes 393224 | tf_op jit(solution)/shard_map/ppermute | solution.py:356
  61.4 16.4 %collective-permute-start.4 = (bf16[64,1024]{1,0:T(8,128)(2,1)S(1)}, bf16[64,1024]{1,0:T(8,128)(2,1)S(1)}, u32[]{:S(2)}, u32[]{:S(2)}) collective-permute-start(bf16[64,1024]{1,0:T(8,128)(2,1)S(1)} %get-tuple-element.45), channel_id=1, source_target_pairs={{0,4},{4,0},{1,5},{5,1},{2,6},{6,2},{3,7},{7,3}} | collective-permute-start | bytes 393224 | tf_op jit(solution)/shard_map/ppermute | solution.py:356
  76.6 5.0 %collective-permute-start.7 = (bf16[64,1024]{1,0:T(8,128)(2,1)S(1)}, bf16[64,1024]{1,0:T(8,128)(2,1)S(1)}, u32[]{:S(2)}, u32[]{:S(2)}) collective-permute-start(bf16[64,1024]{1,0:T(8,128)(2,1)S(1)} %get-tuple-element.60), channel_id=1, source_target_pairs={{0,4},{4,0},{1,5},{5,1},{2,6},{6,2},{3,7},{7,3}} | collective-permute-start | bytes 393224 | tf_op jit(solution)/shard_map/ppermute | solution.py:356
  83.1 14.3 %collective-permute-start.8 = (bf16[256,1024]{1,0:T(8,128)(2,1)}, bf16[256,1024]{1,0:T(8,128)(2,1)S(1)}, u32[]{:S(2)}, u32[]{:S(2)}) collective-permute-start(bf16[256,1024]{1,0:T(8,128)(2,1)} %slice.207), channel_id=1, source_target_pairs={{0,1},{1,0},{2,3},{3,2},{4,5},{5,4},{6,7},{7,6}} | collective-permute-start | bytes 1572872 | tf_op jit(solution)/shard_map/ppermute | solution.py:359
  85.2 11.6 %copy-start.30 = (bf16[1024]{0:T(1024)(128)(2,1)S(1)}, bf16[1024]{0:T(1024)(128)(2,1)}, u32[]{:S(2)}) copy-start(bf16[1024]{0:T(1024)(128)(2,1)} %param.29) | copy-start | bytes 6148
  85.3 12.1 %copy-start.31 = (bf16[2,2048]{1,0:T(2,128)(2,1)S(1)}, bf16[2,2048]{1,0:T(2,128)(2,1)}, u32[]{:S(2)}) copy-start(bf16[2,2048]{1,0:T(2,128)(2,1)} %param.25) | copy-start | bytes 24580
  85.3 15.2 %collective-permute-start.33 = (bf16[256,1024]{1,0:T(8,128)(2,1)}, bf16[256,1024]{1,0:T(8,128)(2,1)}, u32[]{:S(2)}, u32[]{:S(2)}) collective-permute-start(bf16[256,1024]{1,0:T(8,128)(2,1)} %slice.205), channel_id=1, source_target_pairs={{0,1},{1,0},{2,3},{3,2},{4,5},{5,4},{6,7},{7,6}} | collective-permute-start | bytes 1572872 | tf_op jit(solution)/shard_map/ppermute | solution.py:359
  93.5 61.1 %collective-permute-start.16 = (bf16[2,512,256]{2,1,0:T(8,128)(2,1)}, bf16[2,512,256]{2,1,0:T(8,128)(2,1)S(1)}, u32[]{:S(2)}, u32[]{:S(2)}) collective-permute-start(bf16[2,512,256]{2,1,0:T(8,128)(2,1)} %get-tuple-element.63), channel_id=1, source_target_pairs={{0,4},{4,0},{1,5},{5,1},{2,6},{6,2},{3,7},{7,3}} | collective-permute-start | bytes 1572872 | tf_op jit(solution)/shard_map/ppermute | solution.py:356
  93.5 61.1 %collective-permute-start.17 = (bf16[2,512,256]{2,1,0:T(8,128)(2,1)}, bf16[2,512,256]{2,1,0:T(8,128)(2,1)S(1)}, u32[]{:S(2)}, u32[]{:S(2)}) collective-permute-start(bf16[2,512,256]{2,1,0:T(8,128)(2,1)} %get-tuple-element.64), channel_id=1, source_target_pairs={{0,4},{4,0},{1,5},{5,1},{2,6},{6,2},{3,7},{7,3}} | collective-permute-start | bytes 1572872 | tf_op jit(solution)/shard_map/ppermute | solution.py:356
  99.0 9.2 %collective-permute-start.9 = (bf16[128,1024]{1,0:T(8,128)(2,1)S(1)}, bf16[128,1024]{1,0:T(8,128)(2,1)S(1)}, u32[]{:S(2)}, u32[]{:S(2)}) collective-permute-start(bf16[128,1024]{1,0:T(8,128)(2,1)S(1)} %slice.211), channel_id=1, source_target_pairs={{0,2},{1,3},{2,0},{3,1},{4,6},{5,7},{6,4},{7,5}} | collective-permute-start | bytes 786440 | tf_op jit(solution)/shard_map/ppermute | solution.py:362
  101.8 10.6 %collective-permute-start.34 = (bf16[128,1024]{1,0:T(8,128)(2,1)S(1)}, bf16[128,1024]{1,0:T(8,128)(2,1)S(1)}, u32[]{:S(2)}, u32[]{:S(2)}) collective-permute-start(bf16[128,1024]{1,0:T(8,128)(2,1)S(1)} %slice.209), channel_id=1, source_target_pairs={{0,2},{1,3},{2,0},{3,1},{4,6},{5,7},{6,4},{7,5}} | collective-permute-start | bytes 786440 | tf_op jit(solution)/shard_map/ppermute | solution.py:362
  102.4 29.7 %collective-permute-start.51 = (bf16[256,1024]{1,0:T(8,128)(2,1)S(1)}, bf16[256,1024]{1,0:T(8,128)(2,1)S(1)}, u32[]{:S(2)}, u32[]{:S(2)}) collective-permute-start(bf16[256,1024]{1,0:T(8,128)(2,1)S(1)} %pad_maximum_fusion.12), channel_id=1, source_target_pairs={{0,4},{4,0},{1,5},{5,1},{2,6},{6,2},{3,7},{7,3}} | collective-permute-start | bytes 1572872 | tf_op jit(solution)/shard_map/ppermute | solution.py:356
  114.1 16.2 %collective-permute-start.10 = (f32[2,128]{1,0:T(2,128)S(1)}, f32[2,128]{1,0:T(2,128)S(1)}, u32[]{:S(2)}, u32[]{:S(2)}) collective-permute-start(f32[2,128]{1,0:T(2,128)S(1)} %pad_maximum_fusion.13), channel_id=1, source_target_pairs={{0,4},{4,0},{1,5},{5,1},{2,6},{6,2},{3,7},{7,3}} | collective-permute-start | bytes 3080 | tf_op jit(solution)/shard_map/ppermute | solution.py:356
  114.4 15.8 %collective-permute-start.35 = (f32[2,128]{1,0:T(2,128)S(1)}, f32[2,128]{1,0:T(2,128)S(1)}, u32[]{:S(2)}, u32[]{:S(2)}) collective-permute-start(f32[2,128]{1,0:T(2,128)S(1)} %pad_maximum_fusion.15), channel_id=1, source_target_pairs={{0,4},{4,0},{1,5},{5,1},{2,6},{6,2},{3,7},{7,3}} | collective-permute-start | bytes 3080 | tf_op jit(solution)/shard_map/ppermute | solution.py:356
  130.5 7.4 %collective-permute-start.11 = (bf16[128,1024]{1,0:T(8,128)(2,1)S(1)}, bf16[128,1024]{1,0:T(8,128)(2,1)S(1)}, u32[]{:S(2)}, u32[]{:S(2)}) collective-permute-start(bf16[128,1024]{1,0:T(8,128)(2,1)S(1)} %get-tuple-element.118), channel_id=1, source_target_pairs={{0,2},{1,3},{2,0},{3,1},{4,6},{5,7},{6,4},{7,5}} | collective-permute-start | bytes 786440 | tf_op jit(solution)/shard_map/ppermute | solution.py:362
  132.1 19.8 %collective-permute-start.13 = (bf16[128,1024]{1,0:T(8,128)(2,1)S(1)}, bf16[128,1024]{1,0:T(8,128)(2,1)S(1)}, u32[]{:S(2)}, u32[]{:S(2)}) collective-permute-start(bf16[128,1024]{1,0:T(8,128)(2,1)S(1)} %get-tuple-element.118), channel_id=1, source_target_pairs={{0,4},{4,0},{1,5},{5,1},{2,6},{6,2},{3,7},{7,3}} | collective-permute-start | bytes 786440 | tf_op jit(solution)/shard_map/ppermute | solution.py:356
  132.6 19.8 %collective-permute-start.38 = (bf16[128,1024]{1,0:T(8,128)(2,1)S(1)}, bf16[128,1024]{1,0:T(8,128)(2,1)S(1)}, u32[]{:S(2)}, u32[]{:S(2)}) collective-permute-start(bf16[128,1024]{1,0:T(8,128)(2,1)S(1)} %get-tuple-element.117), channel_id=1, source_target_pairs={{0,4},{4,0},{1,5},{5,1},{2,6},{6,2},{3,7},{7,3}} | collective-permute-start | bytes 786440 | tf_op jit(solution)/shard_map/ppermute | solution.py:356
  138.0 15.1 %collective-permute-start.36 = (bf16[128,1024]{1,0:T(8,128)(2,1)S(1)}, bf16[128,1024]{1,0:T(8,128)(2,1)S(1)}, u32[]{:S(2)}, u32[]{:S(2)}) collective-permute-start(bf16[128,1024]{1,0:T(8,128)(2,1)S(1)} %get-tuple-element.117), channel_id=1, source_target_pairs={{0,2},{1,3},{2,0},{3,1},{4,6},{5,7},{6,4},{7,5}} | collective-permute-start | bytes 786440 | tf_op jit(solution)/shard_map/ppermute | solution.py:362
  139.4 12.5 %copy-start.17 = (bf16[2,512,256]{2,1,0:T(8,128)(2,1)S(1)}, bf16[2,512,256]{2,1,0:T(8,128)(2,1)}, u32[]{:S(2)}) copy-start(bf16[2,512,256]{2,1,0:T(8,128)(2,1)} %copy-done.16) | copy-start | bytes 1572868
  151.9 14.8 %collective-permute-start.18 = (bf16[2,512,256]{2,1,0:T(8,128)(2,1)S(1)}, bf16[2,512,256]{2,1,0:T(8,128)(2,1)S(1)}, u32[]{:S(2)}, u32[]{:S(2)}) collective-permute-start(bf16[2,512,256]{2,1,0:T(8,128)(2,1)S(1)} %copy-done.17), channel_id=1, source_target_pairs={{0,4},{4,0},{1,5},{5,1},{2,6},{6,2},{3,7},{7,3}} | collective-permute-start | bytes 1572872 | tf_op jit(solution)/shard_map/ppermute | solution.py:356
  152.5 8.8 %collective-permute-start.14 = (bf16[128,1024]{1,0:T(8,128)(2,1)S(1)}, bf16[128,1024]{1,0:T(8,128)(2,1)S(1)}, u32[]{:S(2)}, u32[]{:S(2)}) collective-permute-start(bf16[128,1024]{1,0:T(8,128)(2,1)S(1)} %collective-permute-done.13), channel_id=1, source_target_pairs={{0,2},{1,3},{2,0},{3,1},{4,6},{5,7},{6,4},{7,5}} | collective-permute-start | bytes 786440 | tf_op jit(solution)/shard_map/ppermute | solution.py:362
  153.1 11.0 %collective-permute-start.39 = (bf16[128,1024]{1,0:T(8,128)(2,1)S(1)}, bf16[128,1024]{1,0:T(8,128)(2,1)S(1)}, u32[]{:S(2)}, u32[]{:S(2)}) collective-permute-start(bf16[128,1024]{1,0:T(8,128)(2,1)S(1)} %collective-permute-done.38), channel_id=1, source_target_pairs={{0,2},{1,3},{2,0},{3,1},{4,6},{5,7},{6,4},{7,5}} | collective-permute-start | bytes 786440 | tf_op jit(solution)/shard_map/ppermute | solution.py:362
  154.5 12.2 %copy-start.13 = (bf16[2,512,256]{2,1,0:T(8,128)(2,1)S(1)}, bf16[2,512,256]{2,1,0:T(8,128)(2,1)}, u32[]{:S(2)}) copy-start(bf16[2,512,256]{2,1,0:T(8,128)(2,1)} %copy-done.12) | copy-start | bytes 1572868
  154.5 12.7 %copy-start.11 = (bf16[2,512,256]{2,1,0:T(8,128)(2,1)S(1)}, bf16[2,512,256]{2,1,0:T(8,128)(2,1)}, u32[]{:S(2)}) copy-start(bf16[2,512,256]{2,1,0:T(8,128)(2,1)} %copy-done.10) | copy-start | bytes 1572868
  154.6 12.7 %collective-permute-start.12 = (bf16[256,1024]{1,0:T(8,128)(2,1)S(1)}, bf16[256,1024]{1,0:T(8,128)(2,1)S(1)}, u32[]{:S(2)}, u32[]{:S(2)}) collective-permute-start(bf16[256,1024]{1,0:T(8,128)(2,1)S(1)} %pad_maximum_fusion.5), channel_id=1, source_target_pairs={{0,1},{1,0},{2,3},{3,2},{4,5},{5,4},{6,7},{7,6}} | collective-permute-start | bytes 1572872 | tf_op jit(solution)/shard_map/ppermute | solution.py:359
  154.7 23.3 %collective-permute-start.19 = (bf16[2,512,256]{2,1,0:T(8,128)(2,1)S(1)}, bf16[2,512,256]{2,1,0:T(8,128)(2,1)S(1)}, u32[]{:S(2)}, u32[]{:S(2)}) collective-permute-start(bf16[2,512,256]{2,1,0:T(8,128)(2,1)S(1)} %copy-done.15), channel_id=1, source_target_pairs={{0,4},{4,0},{1,5},{5,1},{2,6},{6,2},{3,7},{7,3}} | collective-permute-start | bytes 1572872 | tf_op jit(solution)/shard_map/ppermute | solution.py:356
  161.3 17.2 %collective-permute-start.37 = (bf16[256,1024]{1,0:T(8,128)(2,1)S(1)}, bf16[256,1024]{1,0:T(8,128)(2,1)S(1)}, u32[]{:S(2)}, u32[]{:S(2)}) collective-permute-start(bf16[256,1024]{1,0:T(8,128)(2,1)S(1)} %pad_maximum_fusion.8), channel_id=1, source_target_pairs={{0,1},{1,0},{2,3},{3,2},{4,5},{5,4},{6,7},{7,6}} | collective-permute-start | bytes 1572872 | tf_op jit(solution)/shard_map/ppermute | solution.py:359
  161.3 16.7 %copy-start.9 = (bf16[2,512,256]{2,1,0:T(8,128)(2,1)S(1)}, bf16[2,512,256]{2,1,0:T(8,128)(2,1)}, u32[]{:S(2)}) copy-start(bf16[2,512,256]{2,1,0:T(8,128)(2,1)} %copy-done.8) | copy-start | bytes 1572868
  164.1 16.0 %collective-permute-start.15 = (bf16[256,1024]{1,0:T(8,128)(2,1)S(1)}, bf16[256,1024]{1,0:T(8,128)(2,1)S(1)}, u32[]{:S(2)}, u32[]{:S(2)}) collective-permute-start(bf16[256,1024]{1,0:T(8,128)(2,1)S(1)} %pad_maximum_fusion.6), channel_id=1, source_target_pairs={{0,1},{1,0},{2,3},{3,2},{4,5},{5,4},{6,7},{7,6}} | collective-permute-start | bytes 1572872 | tf_op jit(solution)/shard_map/ppermute | solution.py:359
  166.8 22.5 %collective-permute-start.20 = (bf16[2,512,256]{2,1,0:T(8,128)(2,1)S(1)}, bf16[2,512,256]{2,1,0:T(8,128)(2,1)S(1)}, u32[]{:S(2)}, u32[]{:S(2)}) collective-permute-start(bf16[2,512,256]{2,1,0:T(8,128)(2,1)S(1)} %copy-done.13), channel_id=1, source_target_pairs={{0,4},{4,0},{1,5},{5,1},{2,6},{6,2},{3,7},{7,3}} | collective-permute-start | bytes 1572872 | tf_op jit(solution)/shard_map/ppermute | solution.py:356
  167.3 33.2 %collective-permute-start.21 = (bf16[2,512,256]{2,1,0:T(8,128)(2,1)S(1)}, bf16[2,512,256]{2,1,0:T(8,128)(2,1)S(1)}, u32[]{:S(2)}, u32[]{:S(2)}) collective-permute-start(bf16[2,512,256]{2,1,0:T(8,128)(2,1)S(1)} %copy-done.11), channel_id=1, source_target_pairs={{0,4},{4,0},{1,5},{5,1},{2,6},{6,2},{3,7},{7,3}} | collective-permute-start | bytes 1572872 | tf_op jit(solution)/shard_map/ppermute | solution.py:356
  178.0 33.7 %collective-permute-start.22 = (bf16[2,512,256]{2,1,0:T(8,128)(2,1)S(1)}, bf16[2,512,256]{2,1,0:T(8,128)(2,1)S(1)}, u32[]{:S(2)}, u32[]{:S(2)}) collective-permute-start(bf16[2,512,256]{2,1,0:T(8,128)(2,1)S(1)} %copy-done.9), channel_id=1, source_target_pairs={{0,4},{4,0},{1,5},{5,1},{2,6},{6,2},{3,7},{7,3}} | collective-permute-start | bytes 1572872 | tf_op jit(solution)/shard_map/ppermute | solution.py:356
  178.5 44.4 %collective-permute-start.23 = (bf16[2,512,256]{2,1,0:T(8,128)(2,1)S(1)}, bf16[2,512,256]{2,1,0:T(8,128)(2,1)S(1)}, u32[]{:S(2)}, u32[]{:S(2)}) collective-permute-start(bf16[2,512,256]{2,1,0:T(8,128)(2,1)S(1)} %get-tuple-element.70), channel_id=1, source_target_pairs={{0,4},{4,0},{1,5},{5,1},{2,6},{6,2},{3,7},{7,3}} | collective-permute-start | bytes 1572872 | tf_op jit(solution)/shard_map/ppermute | solution.py:356
  180.1 45.0 %collective-permute-start.40 = (bf16[256,1024]{1,0:T(8,128)(2,1)S(1)}, bf16[256,1024]{1,0:T(8,128)(2,1)S(1)}, u32[]{:S(2)}, u32[]{:S(2)}) collective-permute-start(bf16[256,1024]{1,0:T(8,128)(2,1)S(1)} %pad_maximum_fusion.9), channel_id=1, source_target_pairs={{0,1},{1,0},{2,3},{3,2},{4,5},{5,4},{6,7},{7,6}} | collective-permute-start | bytes 1572872 | tf_op jit(solution)/shard_map/ppermute | solution.py:359
  189.2 89.7 %collective-permute-start.50 = (bf16[256,1024]{1,0:T(8,128)(2,1)S(1)}, bf16[256,1024]{1,0:T(8,128)(2,1)S(1)}, u32[]{:S(2)}, u32[]{:S(2)}) collective-permute-start(bf16[256,1024]{1,0:T(8,128)(2,1)S(1)} %pad_maximum_fusion.11), channel_id=1, source_target_pairs={{0,4},{4,0},{1,5},{5,1},{2,6},{6,2},{3,7},{7,3}} | collective-permute-start | bytes 1572872 | tf_op jit(solution)/shard_map/ppermute | solution.py:356
  200.5 39.3 %collective-permute-start.24 = (bf16[512,256]{1,0:T(8,128)(2,1)S(1)}, bf16[512,256]{1,0:T(8,128)(2,1)S(1)}, u32[]{:S(2)}, u32[]{:S(2)}) collective-permute-start(bf16[512,256]{1,0:T(8,128)(2,1)S(1)} %upgate.8), channel_id=1, source_target_pairs={{0,4},{4,0},{1,5},{5,1},{2,6},{6,2},{3,7},{7,3}} | collective-permute-start | bytes 786440 | tf_op jit(solution)/shard_map/ppermute | solution.py:356
  211.7 33.7 %collective-permute-start.25 = (bf16[512,256]{1,0:T(8,128)(2,1)S(1)}, bf16[512,256]{1,0:T(8,128)(2,1)S(1)}, u32[]{:S(2)}, u32[]{:S(2)}) collective-permute-start(bf16[512,256]{1,0:T(8,128)(2,1)S(1)} %upgate.9), channel_id=1, source_target_pairs={{0,4},{4,0},{1,5},{5,1},{2,6},{6,2},{3,7},{7,3}} | collective-permute-start | bytes 786440 | tf_op jit(solution)/shard_map/ppermute | solution.py:356
  222.9 28.1 %collective-permute-start.26 = (bf16[512,256]{1,0:T(8,128)(2,1)S(1)}, bf16[512,256]{1,0:T(8,128)(2,1)S(1)}, u32[]{:S(2)}, u32[]{:S(2)}) collective-permute-start(bf16[512,256]{1,0:T(8,128)(2,1)S(1)} %upgate.10), channel_id=1, source_target_pairs={{0,4},{4,0},{1,5},{5,1},{2,6},{6,2},{3,7},{7,3}} | collective-permute-start | bytes 786440 | tf_op jit(solution)/shard_map/ppermute | solution.py:356
  225.2 31.5 %collective-permute-start.27 = (bf16[512,256]{1,0:T(8,128)(2,1)S(1)}, bf16[512,256]{1,0:T(8,128)(2,1)S(1)}, u32[]{:S(2)}, u32[]{:S(2)}) collective-permute-start(bf16[512,256]{1,0:T(8,128)(2,1)S(1)} %upgate.11), channel_id=1, source_target_pairs={{0,4},{4,0},{1,5},{5,1},{2,6},{6,2},{3,7},{7,3}} | collective-permute-start | bytes 786440 | tf_op jit(solution)/shard_map/ppermute | solution.py:356
  232.0 25.2 %copy-start.32 = (bf16[2048,1024]{1,0:T(8,128)(2,1)S(1)}, bf16[2048,1024]{1,0:T(8,128)(2,1)}, u32[]{:S(2)}) copy-start(bf16[2048,1024]{1,0:T(8,128)(2,1)} %param.26) | copy-start | bytes 12582916
  239.8 22.5 %collective-permute-start.41 = (bf16[512,256]{1,0:T(8,128)(2,1)S(1)}, bf16[512,256]{1,0:T(8,128)(2,1)S(1)}, u32[]{:S(2)}, u32[]{:S(2)}) collective-permute-start(bf16[512,256]{1,0:T(8,128)(2,1)S(1)} %upgate.12), channel_id=1, source_target_pairs={{0,4},{4,0},{1,5},{5,1},{2,6},{6,2},{3,7},{7,3}} | collective-permute-start | bytes 786440 | tf_op jit(solution)/shard_map/ppermute | solution.py:356
  245.4 22.5 %collective-permute-start.42 = (bf16[512,256]{1,0:T(8,128)(2,1)S(1)}, bf16[512,256]{1,0:T(8,128)(2,1)S(1)}, u32[]{:S(2)}, u32[]{:S(2)}) collective-permute-start(bf16[512,256]{1,0:T(8,128)(2,1)S(1)} %upgate.13), channel_id=1, source_target_pairs={{0,4},{4,0},{1,5},{5,1},{2,6},{6,2},{3,7},{7,3}} | collective-permute-start | bytes 786440 | tf_op jit(solution)/shard_map/ppermute | solution.py:356
  251.0 22.4 %collective-permute-start.43 = (bf16[512,256]{1,0:T(8,128)(2,1)S(1)}, bf16[512,256]{1,0:T(8,128)(2,1)S(1)}, u32[]{:S(2)}, u32[]{:S(2)}) collective-permute-start(bf16[512,256]{1,0:T(8,128)(2,1)S(1)} %upgate.14), channel_id=1, source_target_pairs={{0,4},{4,0},{1,5},{5,1},{2,6},{6,2},{3,7},{7,3}} | collective-permute-start | bytes 786440 | tf_op jit(solution)/shard_map/ppermute | solution.py:356
  256.6 19.6 %collective-permute-start.44 = (bf16[512,256]{1,0:T(8,128)(2,1)S(1)}, bf16[512,256]{1,0:T(8,128)(2,1)S(1)}, u32[]{:S(2)}, u32[]{:S(2)}) collective-permute-start(bf16[512,256]{1,0:T(8,128)(2,1)S(1)} %upgate.15), channel_id=1, source_target_pairs={{0,4},{4,0},{1,5},{5,1},{2,6},{6,2},{3,7},{7,3}} | collective-permute-start | bytes 786440 | tf_op jit(solution)/shard_map/ppermute | solution.py:356
  262.3 16.7 %collective-permute-start.28 = (bf16[256,1024]{1,0:T(8,128)(2,1)S(1)}, bf16[256,1024]{1,0:T(8,128)(2,1)S(1)}, u32[]{:S(2)}, u32[]{:S(2)}) collective-permute-start(bf16[256,1024]{1,0:T(8,128)(2,1)S(1)} %slice.206), channel_id=1, source_target_pairs={{0,1},{1,0},{2,3},{3,2},{4,5},{5,4},{6,7},{7,6}} | collective-permute-start | bytes 1572872 | tf_op jit(solution)/shard_map/ppermute | solution.py:359
  278.8 1.9 collective-permute-start.45
  279.1 14.8 %collective-permute-start.29 = (bf16[128,1024]{1,0:T(8,128)(2,1)S(1)}, bf16[128,1024]{1,0:T(8,128)(2,1)S(1)}, u32[]{:S(2)}, u32[]{:S(2)}) collective-permute-start(bf16[128,1024]{1,0:T(8,128)(2,1)S(1)} %slice.210), channel_id=1, source_target_pairs={{0,2},{1,3},{2,0},{3,1},{4,6},{5,7},{6,4},{7,5}} | collective-permute-start | bytes 786440 | tf_op jit(solution)/shard_map/ppermute | solution.py:362
  281.0 13.0 %collective-permute-start.46 = (bf16[128,1024]{1,0:T(8,128)(2,1)S(1)}, bf16[128,1024]{1,0:T(8,128)(2,1)S(1)}, u32[]{:S(2)}, u32[]{:S(2)}) collective-permute-start(bf16[128,1024]{1,0:T(8,128)(2,1)S(1)} %slice.208), channel_id=1, source_target_pairs={{0,2},{1,3},{2,0},{3,1},{4,6},{5,7},{6,4},{7,5}} | collective-permute-start | bytes 786440 | tf_op jit(solution)/shard_map/ppermute | solution.py:362
  281.6 12.4 %copy-start.23 = (f32[1024]{0:T(1024)S(1)}, f32[1024]{0:T(1024)}, u32[]{:S(2)}) copy-start(f32[1024]{0:T(1024)} %convert_element_type.95) | copy-start | bytes 12292
  294.5 3.6 %collective-permute-start.30 = (f32[2,128]{1,0:T(2,128)S(1)}, f32[2,128]{1,0:T(2,128)S(1)}, u32[]{:S(2)}, u32[]{:S(2)}) collective-permute-start(f32[2,128]{1,0:T(2,128)S(1)} %pad_maximum_fusion.14), channel_id=1, source_target_pairs={{0,4},{4,0},{1,5},{5,1},{2,6},{6,2},{3,7},{7,3}} | collective-permute-start | bytes 3080 | tf_op jit(solution)/shard_map/ppermute | solution.py:356
  295.6 3.6 %collective-permute-start.47 = (f32[2,128]{1,0:T(2,128)S(1)}, f32[2,128]{1,0:T(2,128)S(1)}, u32[]{:S(2)}, u32[]{:S(2)}) collective-permute-start(f32[2,128]{1,0:T(2,128)S(1)} %pad_maximum_fusion.16), channel_id=1, source_target_pairs={{0,4},{4,0},{1,5},{5,1},{2,6},{6,2},{3,7},{7,3}} | collective-permute-start | bytes 3080 | tf_op jit(solution)/shard_map/ppermute | solution.py:356
  299.5 14.4 %collective-permute-start.48 = (bf16[128,1024]{1,0:T(8,128)(2,1)S(1)}, bf16[128,1024]{1,0:T(8,128)(2,1)S(1)}, u32[]{:S(2)}, u32[]{:S(2)}) collective-permute-start(bf16[128,1024]{1,0:T(8,128)(2,1)S(1)} %get-tuple-element.115), channel_id=1, source_target_pairs={{0,2},{1,3},{2,0},{3,1},{4,6},{5,7},{6,4},{7,5}} | collective-permute-start | bytes 786440 | tf_op jit(solution)/shard_map/ppermute | solution.py:362
  300.7 13.3 %collective-permute-start.31 = (bf16[128,1024]{1,0:T(8,128)(2,1)S(1)}, bf16[128,1024]{1,0:T(8,128)(2,1)S(1)}, u32[]{:S(2)}, u32[]{:S(2)}) collective-permute-start(bf16[128,1024]{1,0:T(8,128)(2,1)S(1)} %get-tuple-element.116), channel_id=1, source_target_pairs={{0,2},{1,3},{2,0},{3,1},{4,6},{5,7},{6,4},{7,5}} | collective-permute-start | bytes 786440 | tf_op jit(solution)/shard_map/ppermute | solution.py:362
  314.0 13.0 %collective-permute-start.49 = (bf16[256,1024]{1,0:T(8,128)(2,1)S(1)}, bf16[256,1024]{1,0:T(8,128)(2,1)S(1)}, u32[]{:S(2)}, u32[]{:S(2)}) collective-permute-start(bf16[256,1024]{1,0:T(8,128)(2,1)S(1)} %pad_maximum_fusion.10), channel_id=1, source_target_pairs={{0,1},{1,0},{2,3},{3,2},{4,5},{5,4},{6,7},{7,6}} | collective-permute-start | bytes 1572872 | tf_op jit(solution)/shard_map/ppermute | solution.py:359
  314.0 13.0 %collective-permute-start.32 = (bf16[256,1024]{1,0:T(8,128)(2,1)S(1)}, bf16[256,1024]{1,0:T(8,128)(2,1)S(1)}, u32[]{:S(2)}, u32[]{:S(2)}) collective-permute-start(bf16[256,1024]{1,0:T(8,128)(2,1)S(1)} %pad_maximum_fusion.7), channel_id=1, source_target_pairs={{0,1},{1,0},{2,3},{3,2},{4,5},{5,4},{6,7},{7,6}} | collective-permute-start | bytes 1572872 | tf_op jit(solution)/shard_map/ppermute | solution.py:359
  (23 other events, 108.0 us)
